TPU v7x, 128 devices: a whole 4x4x4 slice. The times are simulated.
128 devices in a mesh: dp: 32 (over x, y, core), mp: 4 (over z).
Axes of the slice: x: 4, y: 4, z: 4, core: 2. Of those that a mesh axis runs over, the one named last changes fastest.
Arguments:
- slab_values: bfloat16 [128, 128, 2048], P(('dp', 'mp')), may hold values from -6 to 6
- row_ids: int32 [128, 128, 32], P(('dp', 'mp')), may hold values from 0 to 4095, as said below
- peer_counts: int32 [128, 128], P(('dp', 'mp')), may hold values from 1 to 32, as said below
- lookup_slots: int32 [32768, 16], P(('dp', 'mp')), may hold values from 0 to 4095, as said below
- labels: int32 [32768], P('dp'), may hold values 0 or 1
- sample_weight: float32 [32768], P('dp'), may hold values from 0.3 to 9
- weight_in: bfloat16 [1024, 8192], P(None, 'mp'), may hold values from -0.1875 to 0.1875
- bias_in: float32 [8192], P('mp'), may hold values from -3 to 3
- weight_out: bfloat16 [8192], P('mp'), may hold values from -0.0625 to 0.0625
- dense_accum: float32 [1024, 8192], P('dp', 'mp'), may hold values from 1e-08 to 1e-06
- table_rows: float32 [524288, 64], P(('dp', 'mp')), may hold values from -0.12 to 0.12
- table_accum: float32 [524288], P(('dp', 'mp')), may hold values from 1e-12 to 1e-05
Outputs:
- weight_new: bfloat16 [1024, 8192], P(None, 'mp')
- accum_new: float32 [1024, 8192], P('dp', 'mp')
- table_new: float32 [524288, 64], P(('dp', 'mp'))
- table_accum_new: float32 [524288], P(('dp', 'mp'))
Inputs may be any that keep to these rules, and one draw needn't show every extreme that they name: `row_ids`: the first peer_counts entries of each device's list for an owner are distinct rows of that owner's shard. `peer_counts`: some owner has 32 touched rows on every device, and some device has 32 touched rows of every owner. `lookup_slots`: below the sum of that device's peer_counts; every device has a lookup of its last touched row.
All inputs are finite; a program needn't handle non-finite values. No bound on the sum of `labels` on one device may be relied on, other than what follows from the above.
Results may differ from a plain program's by a relative error of at most 0.0034.
Values may be sent and summed in bfloat16 or wider, within the bound.
A program may use at most 128 MiB of HBM per device.

v0:
```python
import functools

import jax
import jax.numpy as jnp
from jax import lax
from jax.sharding import Mesh
from jax.sharding import PartitionSpec as P

DP = ("dp_0", "dp_1", "dp_2")
DP_MP = ("dp_0", "dp_1", "dp_2", "mp")


clip_norm = 1.0
dense_rate = 0.02
table_rate = 0.5
adagrad_eps = 1e-10


def laid_out(pieces, dim):
    dims = list(pieces.shape[1:])
    dims[dim] *= pieces.shape[0]
    return jnp.moveaxis(pieces, 0, dim).reshape(dims)


def from_everyone(shard, axis):
    length = lax.axis_size(axis)
    return lax.all_to_all(
        jnp.broadcast_to(shard[None], (length, *shard.shape)), axis, 0, 0, tiled=True
    )


def gather_directly(shard, axis, dim):
    return laid_out(from_everyone(shard, axis), dim)


def of_everyone(shard, axis):
    return from_everyone(shard, axis).sum(axis=0)


def in_blocks(shard, dim, length):
    dims = shard.shape
    pieces = shard.reshape(*dims[:dim], length, dims[dim] // length, *dims[dim + 1 :])
    return jnp.moveaxis(pieces, dim, 0)


def sum_at_owner(shard, axis, dim):
    pieces = in_blocks(shard, dim, lax.axis_size(axis))
    arrived = lax.all_to_all(pieces, axis, split_axis=0, concat_axis=0, tiled=True)
    return arrived.sum(axis=0)


def together(arrays, axis):
    vector, at, finished = (jnp.concatenate([a.reshape(-1) for a in arrays]), 0, [])
    running = of_everyone(vector, axis)
    for a in arrays:
        finished.append(running[at : at + a.size].reshape(a.shape))
        at += a.size
    return tuple(finished)


def over_axes(shard, axes):
    return functools.reduce(lax.psum, axes, shard)


def in_one_piece(arrays, axis, split_dim, concat_dim, along):
    widths = [a.shape[along] for a in arrays]
    both = jnp.concatenate(arrays, axis=along)
    whole = lax.all_to_all(both, axis, split_axis=split_dim, concat_axis=concat_dim, tiled=True)
    return tuple(jnp.split(whole, [sum(widths[:k]) for k in range(1, len(widths))], axis=along))


def slot_index(compact, counts, capacity):
    slot_ends = jnp.cumsum(counts)
    owner_index = jnp.sum((compact[..., None] >= slot_ends).astype(jnp.int32), axis=-1)
    slot_starts = slot_ends - counts
    owner_match = owner_index[..., None] == jnp.arange(counts.shape[0], dtype=jnp.int32)
    owner_begin = jnp.sum(jnp.where(owner_match, slot_starts, 0), axis=-1)
    return owner_index * capacity + compact - owner_begin


def body(
    slab_values,
    row_ids,
    peer_counts,
    lookup_slots,
    labels,
    sample_weight,
    weight_in,
    bias_in,
    weight_out,
    dense_accum,
    table_rows,
    table_accum,
):
    peers = peer_counts.shape[1]
    capacity = row_ids.shape[2]
    emb_width = slab_values.shape[2] // capacity
    batch = lookup_slots.shape[0]
    features = lookup_slots.shape[1]
    index = slot_index(lookup_slots, peer_counts[0], capacity)
    slab_view = slab_values[0].reshape(peers * capacity, emb_width)
    pooled = slab_view[index].reshape(batch, features * emb_width)
    group = gather_directly(pooled, "mp", 0)
    act = jnp.dot(group, weight_in, preferred_element_type=jnp.float32) + bias_in
    hidden = jax.nn.silu(act).astype(jnp.bfloat16)
    logit = of_everyone(jnp.dot(hidden, weight_out, preferred_element_type=jnp.float32), "mp")
    dlogit = sample_weight * (jax.nn.sigmoid(logit) - labels.astype(jnp.float32))
    sigma = jax.nn.sigmoid(act)
    dact = (
        dlogit[:, None]
        * weight_out.astype(jnp.float32)[None, :]
        * sigma
        * (1.0 + act * (1.0 - sigma))
    ).astype(jnp.bfloat16)
    dpooled = sum_at_owner(
        lax.dot_general(
            dact, weight_in, (((1,), (1,)), ((), ())), preferred_element_type=jnp.float32
        ),
        "mp",
        0,
    )
    slot_grad = jax.ops.segment_sum(
        dpooled.reshape(batch * features, emb_width),
        index.reshape(-1),
        num_segments=peers * capacity,
    )
    grad_in = lax.dot_general(
        group, dact, (((0,), (0,)), ((), ())), preferred_element_type=jnp.float32
    )
    grad_bias = jnp.sum(dact.astype(jnp.float32), axis=0)
    grad_out = jnp.dot(dlogit, hidden.astype(jnp.float32))
    first_group = (lax.axis_index(DP) == 0).astype(jnp.float32)
    own_rows = dense_accum.shape[0]
    row_start = lax.axis_index(DP) * own_rows
    grad_rows = lax.psum_scatter(grad_in, DP, scatter_dimension=0, tiled=True)
    grad_bias, grad_out = together((grad_bias, grad_out), DP)
    dense_square = jnp.sum(grad_rows * grad_rows)
    dense_square = dense_square + first_group * (
        jnp.sum(grad_bias * grad_bias) + jnp.sum(grad_out * grad_out)
    )
    total = over_axes(dense_square + jnp.sum(slot_grad * slot_grad), DP_MP)
    scale = clip_norm / jnp.maximum(jnp.sqrt(total), clip_norm)
    clipped = scale * grad_rows
    accum_new = dense_accum + clipped * clipped
    weight_part = lax.dynamic_slice_in_dim(weight_in, row_start, own_rows, 0).astype(jnp.float32)
    updated = (weight_part - dense_rate * clipped / (jnp.sqrt(accum_new) + adagrad_eps)).astype(
        jnp.bfloat16
    )
    weight_new = lax.all_gather(updated, DP, axis=0, tiled=True)
    row_values = row_ids[0].astype(jnp.float32)
    outgoing = (scale * slot_grad).reshape(peers, capacity * emb_width)
    arrived, arrived_rows = in_one_piece((outgoing, row_values), DP_MP, 0, 0, 1)
    received = jax.ops.segment_sum(
        arrived.reshape(-1, emb_width),
        arrived_rows.reshape(-1).astype(jnp.int32),
        num_segments=table_rows.shape[0],
    )
    table_accum_new = table_accum + jnp.mean(received * received, axis=1)
    table_new = table_rows - table_rate * received / (
        jnp.sqrt(table_accum_new)[:, None] + adagrad_eps
    )
    return (weight_new, accum_new, table_new, table_accum_new)


def solution(mesh):
    torus = Mesh(mesh.devices.reshape(4, 4, 2, mesh.shape["mp"]), ("dp_0", "dp_1", "dp_2", "mp"))
    placed = (
        P(DP_MP, None, None),
        P(DP_MP, None, None),
        P(DP_MP, None),
        P(DP_MP, None),
        P(DP),
        P(DP),
        P(None, "mp"),
        P("mp"),
        P("mp"),
        P(DP, "mp"),
        P(DP_MP, None),
        P(DP_MP),
    )
    return jax.shard_map(
        body,
        mesh=torus,
        in_specs=placed,
        out_specs=(P(None, "mp"), P(DP, "mp"), P(DP_MP, None), P(DP_MP)),
        check_vma=False,
    )
```

profile of v0, /device:TPU:1, one launch (start us, length us, event | category | flops | bytes accessed | tf_op | source)
XLA Modules:
  0.0 327.6 jit_solution(4526414927687475050)
XLA Ops:
  9.8 5.7 %convert_reduce_fusion.1 = s32[256,16]{1,0:T(8,128)S(1)} fusion(s32[128]{0:T(128)S(1)} %reduce.2, s32[256,16]{1,0:T(8,128)S(1)} %copy.59), kind=kLoop, calls=%fused_computation.12 | loop fusion | flops 1568768 | bytes 33280 | tf_op jit(solution)/shard_map/reduce_sum | solution.py:74
  15.5 5.7 %select_reduce_fusion = s32[256,16]{1,0:T(8,128)S(1)} fusion(s32[128]{0:T(128)S(1)} %bitcast_subtract_fusion, s32[256,16]{1,0:T(8,128)S(1)} %convert_reduce_fusion.1), kind=kLoop, calls=%fused_computation.10 | loop fusion | flops 1568768 | bytes 33280 | tf_op jit(solution)/shard_map/reduce_sum | solution.py:77
  22.5 12.1 %gather_fusion = bf16[4096,64]{1,0:T(8,128)(2,1)S(1)} fusion(bf16[4096,64]{1,0:T(8,128)(2,1)S(1)} %reshape_squeeze.3, s32[4096]{0:T(1024)S(1)} %broadcast_clamp_fusion), kind=kCustom, calls=%fused_computation | custom fusion | bytes 1064960 | tf_op jit(solution)/shard_map/gather | solution.py:102
  36.9 6.0 %all-to-all-start = ((bf16[4,256,1024]{2,1,0:T(8,128)(2,1)}), bf16[4,256,1024]{2,1,0:T(8,128)(2,1)S(1)}, u32[]{:S(2)}, u32[]{:S(2)}) async-start(bf16[4,256,1024]{2,1,0:T(8,128)(2,1)} %broadcast_in_dim.22), calls=%async_computation | async-start | bytes 4194304 | tf_op jit(solution)/shard_map/all_to_all | solution.py:27
  42.9 25.5 %all-to-all-done = bf16[4,256,1024]{2,1,0:T(8,128)(2,1)S(1)} async-done(((bf16[4,256,1024]{2,1,0:T(8,128)(2,1)}), bf16[4,256,1024]{2,1,0:T(8,128)(2,1)S(1)}, u32[]{:S(2)}, u32[]{:S(2)}) %all-to-all-start) | async-done | bytes 2097184 | tf_op jit(solution)/shard_map/all_to_all | solution.py:27
  68.4 9.7 %multiply_convert_fusion.1 = (bf16[1024,2048]{1,0:T(8,128)(2,1)S(1)}, f32[1024,2048]{1,0:T(8,128)}) fusion(f32[2048]{0:T(1024)S(1)} %copy-done.9, bf16[1024,1024]{1,0:T(8,128)(2,1)S(1)} %bitcast.26, bf16[1024,2048]{1,0:T(8,128)(2,1)} %param.18), kind=kOutput, calls=%fused_computation.5 | convolution fusion | flops 4307550208 | bytes 18882560 | tf_op jit(solution)/shard_map/dot_general | solution.py:104
  80.7 3.3 all-to-all-start.1
  84.2 3.9 %all-to-all-done.1 = f32[4,1,1024]{2,1,0:T(1,128)S(1)} async-done(((f32[4,1,1024]{2,1,0:T(1,128)}), f32[4,1,1024]{2,1,0:T(1,128)S(1)}, u32[]{:S(2)}, u32[]{:S(2)}) %all-to-all-start.1) | async-done | bytes 16416 | tf_op jit(solution)/shard_map/all_to_all | solution.py:27
  88.2 6.0 %convert_reduce_fusion = (f32[2048]{0:T(1024)S(1)}, bf16[1024,2048]{1,0:T(8,128)(2,1)S(1)}) fusion(f32[1024,2048]{1,0:T(8,128)} %get-tuple-element.35, f32[2048]{0:T(1024)S(1)} %copy-done.9, f32[2048]{0:T(1024)S(1)} %convert_element_type.49, f32[1024]{0:T(1024)S(1)} %subtract_multiply_fusion), kind=kLoop, calls=%fused_computation.3 | loop fusion | flops 27260928 | bytes 12611584 | tf_op jit(solution)/shard_map/reduce_sum | solution.py:130
  94.2 2.0 copy-done.2
  96.1 6.7 %fusion.7 = f32[1024,2048]{1,0:T(8,128)} fusion(bf16[1024,1024]{1,0:T(8,128)(2,1)S(1)} %bitcast.27, bf16[1024,2048]{1,0:T(8,128)(2,1)S(1)} %get-tuple-element.31), kind=kOutput, calls=%fused_computation.37 | convolution fusion | flops 4294967296 | bytes 14680064 | tf_op jit(solution)/shard_map/dot_general | solution.py:127
  102.9 2.8 fusion.8
  107.0 10.1 %all-to-all-start.2 = ((f32[32,1,4096]{2,1,0:T(1,128)}), f32[32,1,4096]{2,1,0:T(1,128)S(1)}, u32[]{:S(2)}, u32[]{:S(2)}) async-start(f32[32,1,4096]{2,1,0:T(1,128)} %broadcast_in_dim.24), calls=%async_computation.3 | async-start | bytes 1048576 | tf_op jit(solution)/shard_map/all_to_all | solution.py:27
  117.1 10.4 %fusion.9 = f32[1024,1024]{1,0:T(8,128)} fusion(bf16[1024,2048]{1,0:T(8,128)(2,1)} %copy-done.2, bf16[1024,2048]{1,0:T(8,128)(2,1)} %param.18), kind=kOutput, calls=%fused_computation.39 | convolution fusion | flops 4294967296 | bytes 12582912 | tf_op jit(solution)/shard_map/dot_general | solution.py:116
  128.7 5.0 %all-to-all-start.3 = ((f32[4,256,1024]{2,1,0:T(8,128)}), f32[4,256,1024]{2,1,0:T(8,128)}, u32[]{:S(2)}, u32[]{:S(2)}) async-start(f32[4,256,1024]{2,1,0:T(8,128)} %bitcast.25), calls=%async_computation.4 | async-start | bytes 8388608 | tf_op jit(solution)/shard_map/all_to_all | solution.py:48
  136.3 46.6 %all-to-all-done.3 = f32[4,256,1024]{2,1,0:T(8,128)} async-done(((f32[4,256,1024]{2,1,0:T(8,128)}), f32[4,256,1024]{2,1,0:T(8,128)}, u32[]{:S(2)}, u32[]{:S(2)}) %all-to-all-start.3) | async-done | bytes 4194336 | tf_op jit(solution)/shard_map/all_to_all | solution.py:48
  182.9 2.9 reduce_sum.107
  185.8 1.9 reshape.101
  187.7 23.2 %scatter_custom_fusion = f32[4096,64]{1,0:T(8,128)S(1)} fusion(s32[4096]{0:T(1024)S(1)} %reshape.99, f32[4096,64]{1,0:T(8,128)} %reshape.101, f32[]{:T(128)} %constant.14.clone.1), kind=kCustom, calls=%fused_computation.17 | custom fusion | flops 262144 | bytes 1049088 | tf_op jit(solution)/shard_map/scatter-add | solution.py:122
  215.0 7.1 %psum.28 = f32[]{:T(128)} all-reduce(f32[]{:T(128)S(6)} %add.94), channel_id=1, replica_groups=mesh['dp_0'=4,'dp_1'=4,'dp_2'=2,'mp'=4] {'dp_0'}, use_global_device_ids=true, to_apply=%region_13.14 | all-reduce | flops 1 | bytes 8 | tf_op jit(solution)/shard_map/psum | solution.py:62
  222.0 9.0 %psum.29 = f32[]{:T(128)} all-reduce(f32[]{:T(128)} %psum.28), channel_id=1, replica_groups=mesh['dp_0'=4,'dp_1'=4,'dp_2'=2,'mp'=4] {'dp_1'}, use_global_device_ids=true, to_apply=%region_14.15 | all-reduce | flops 1 | bytes 8 | tf_op jit(solution)/shard_map/psum | solution.py:62
  231.0 8.1 %psum.30 = f32[]{:T(128)} all-reduce(f32[]{:T(128)} %psum.29), channel_id=1, replica_groups=mesh['dp_0'=4,'dp_1'=4,'dp_2'=2,'mp'=4] {'dp_2'}, use_global_device_ids=true, to_apply=%region_15.16 | all-reduce | flops 1 | bytes 8 | tf_op jit(solution)/shard_map/psum | solution.py:62
  239.1 7.4 %psum.31 = f32[]{:T(128)} all-reduce(f32[]{:T(128)} %psum.30), channel_id=1, replica_groups=mesh['dp_0'=4,'dp_1'=4,'dp_2'=2,'mp'=4] {'mp'}, use_global_device_ids=true, to_apply=%region_16.17 | all-reduce | flops 1 | bytes 8 | tf_op jit(solution)/shard_map/psum | solution.py:62
  250.7 2.1 reshape.87
  252.9 2.1 copy.65
  255.1 5.8 %all-to-all-start.4 = ((f32[128,1,2080]{2,1,0:T(1,128)}), f32[128,1,2080]{2,1,0:T(1,128)S(1)}, u32[]{:S(2)}, u32[]{:S(2)}) async-start(f32[128,1,2080]{2,1,0:T(1,128)} %copy.65), calls=%async_computation.5 | async-start | bytes 2228224 | tf_op jit(solution)/shard_map/all_to_all | solution.py:68
  260.9 1.9 copy.69
  262.8 19.3 %all-to-all-done.4 = f32[128,1,2080]{2,1,0:T(1,128)S(1)} async-done(((f32[128,1,2080]{2,1,0:T(1,128)}), f32[128,1,2080]{2,1,0:T(1,128)S(1)}, u32[]{:S(2)}, u32[]{:S(2)}) %all-to-all-start.4) | async-done | bytes 1064992 | tf_op jit(solution)/shard_map/all_to_all | solution.py:68
  283.9 2.2 reshape.109
  286.3 23.2 %scatter_custom_fusion.1 = f32[4096,64]{1,0:T(8,128)S(1)} fusion(s32[4096]{0:T(1024)S(1)} %reshape.107, f32[4096,64]{1,0:T(8,128)} %reshape.109, f32[]{:T(128)} %constant.14.clone.1), kind=kCustom, calls=%fused_computation.15 | custom fusion | flops 262144 | bytes 1049088 | tf_op jit(solution)/shard_map/scatter-add | solution.py:153
  312.8 3.1 copy.70
  315.9 4.8 %copy.76 = bf16[1024,2048]{1,0:T(8,128)(2,1)} copy(bf16[1024,2048]{1,0:T(8,128)(2,1)} %all-gather.2.cloned.1.call-done) | data formatting | bytes 8388608
  (68 shorter events, 24.4 us)
Async XLA Ops:
  7.2 14.2 %copy-start.4 = (bf16[1,128,2048]{2,1,0:T(8,128)(2,1)S(1)}, bf16[1,128,2048]{2,1,0:T(8,128)(2,1)}, u32[]{:S(2)}) copy-start(bf16[1,128,2048]{2,1,0:T(8,128)(2,1)} %param.12) | copy-start | bytes 1572868
  36.9 6.0 %copy-start.7 = (bf16[2048]{0:T(1024)(128)(2,1)S(1)}, bf16[2048]{0:T(1024)(128)(2,1)}, u32[]{:S(2)}) copy-start(bf16[2048]{0:T(1024)(128)(2,1)} %param.20) | copy-start | bytes 12292
  36.9 31.5 %copy-start.9 = (f32[2048]{0:T(1024)S(1)}, f32[2048]{0:T(1024)}, u32[]{:S(2)}) copy-start(f32[2048]{0:T(1024)} %param.19) | copy-start | bytes 24580
  36.9 31.5 %all-to-all-start = ((bf16[4,256,1024]{2,1,0:T(8,128)(2,1)}), bf16[4,256,1024]{2,1,0:T(8,128)(2,1)S(1)}, u32[]{:S(2)}, u32[]{:S(2)}) async-start(bf16[4,256,1024]{2,1,0:T(8,128)(2,1)} %broadcast_in_dim.22), calls=%async_computation | async-start | bytes 4194304 | tf_op jit(solution)/shard_map/all_to_all | solution.py:27
  78.1 2.0 copy-start
  78.1 10.1 %copy-start.10 = (f32[1024]{0:T(1024)S(1)}, f32[1024]{0:T(1024)}, u32[]{:S(2)}) copy-start(f32[1024]{0:T(1024)} %param.17) | copy-start | bytes 12292
  78.1 10.1 %copy-start.11 = (s32[1024]{0:T(1024)S(1)}, s32[1024]{0:T(1024)}, u32[]{:S(2)}) copy-start(s32[1024]{0:T(1024)} %param.16) | copy-start | bytes 12292
  80.7 7.4 %all-to-all-start.1 = ((f32[4,1,1024]{2,1,0:T(1,128)}), f32[4,1,1024]{2,1,0:T(1,128)S(1)}, u32[]{:S(2)}, u32[]{:S(2)}) async-start(f32[4,1,1024]{2,1,0:T(1,128)} %broadcast_in_dim.23), calls=%async_computation.1 | async-start | bytes 32768 | tf_op jit(solution)/shard_map/all_to_all | solution.py:27
  83.9 128.1 %reduce-scatter.2.cloned.1.call-start = ((), (), s32[]{:S(2)}) async-start(), calls=%async_computation.6 | async-start | bytes 8650752 | tf_op jit(solution)/shard_map/reduce_scatter | solution.py:135
  94.2 2.0 copy-start.2
  107.0 21.7 %all-to-all-start.2 = ((f32[32,1,4096]{2,1,0:T(1,128)}), f32[32,1,4096]{2,1,0:T(1,128)S(1)}, u32[]{:S(2)}, u32[]{:S(2)}) async-start(f32[32,1,4096]{2,1,0:T(1,128)} %broadcast_in_dim.24), calls=%async_computation.3 | async-start | bytes 1048576 | tf_op jit(solution)/shard_map/all_to_all | solution.py:27
  128.7 54.3 %all-to-all-start.3 = ((f32[4,256,1024]{2,1,0:T(8,128)}), f32[4,256,1024]{2,1,0:T(8,128)}, u32[]{:S(2)}, u32[]{:S(2)}) async-start(f32[4,256,1024]{2,1,0:T(8,128)} %bitcast.25), calls=%async_computation.4 | async-start | bytes 8388608 | tf_op jit(solution)/shard_map/all_to_all | solution.py:48
  133.7 182.3 %all-gather.2.cloned.1.call-start = ((), (), s32[]{:S(2)}) async-start(), calls=%async_computation.7 | async-start | bytes 4325376 | tf_op jit(solution)/shard_map/all_gather | solution.py:149
  187.7 59.6 %copy-start.5 = (f32[32,2048]{1,0:T(8,128)S(1)}, f32[32,2048]{1,0:T(8,128)}, u32[]{:S(2)}) copy-start(f32[32,2048]{1,0:T(8,128)} %param.21) | copy-start | bytes 786436
  210.9 38.3 %copy-start.6 = (s32[1,128,32]{1,2,0:T(8,128)S(1)}, s32[1,128,32]{1,2,0:T(8,128)}, u32[]{:S(2)}) copy-start(s32[1,128,32]{1,2,0:T(8,128)} %param.13) | copy-start | bytes 49156
  252.9 7.9 %copy-start.3 = (f32[4096,64]{0,1:T(8,128)S(1)}, f32[4096,64]{0,1:T(8,128)}, u32[]{:S(2)}) copy-start(f32[4096,64]{0,1:T(8,128)} %param.22) | copy-start | bytes 3145732
  255.1 27.0 %all-to-all-start.4 = ((f32[128,1,2080]{2,1,0:T(1,128)}), f32[128,1,2080]{2,1,0:T(1,128)S(1)}, u32[]{:S(2)}, u32[]{:S(2)}) async-start(f32[128,1,2080]{2,1,0:T(1,128)} %copy.65), calls=%async_computation.5 | async-start | bytes 2228224 | tf_op jit(solution)/shard_map/all_to_all | solution.py:68
  286.3 23.9 %copy-start.8 = (f32[4096]{0:T(1024)S(1)}, f32[4096]{0:T(1024)}, u32[]{:S(2)}) copy-start(f32[4096]{0:T(1024)} %param.23) | copy-start | bytes 49156
  309.5 1.6 copy-start.1
Sparse Core Ops, SparseCore 0:
  103.0 92.6 reduce-scatter.1
  249.3 48.8 all-gather.1
where the time goes:
time: 329 us; the launch traced here: 328 us
  waiting for transfers between devices  96.5 us (29%)
  other arithmetic  77.7 us (24%)
  local copies, waits for them, and re-layouts  42.7 us (13%)
  blocking collectives  31.6 us (10%)
  matrix products  30.9 us (9%)
  starting transfers between devices  30.5 us (9%)
  between operations  17.7 us (5%)
    all_to_all x1, waiting for transfers between devices, sum_at_owner(): lax.all_to_all(pieces, axis, split_axis=0, concat_axis=0, tiled=True)  46.6 us
    psum x4, blocking collectives, over_axes(): return functools.reduce(lax.psum, axes, shard)  31.6 us
    all_to_all x3, waiting for transfers between devices, from_everyone(): lax.all_to_all(jnp.broadcast_to(shard[None], (length, *shard.shape)), axi...  30.6 us
    scatter-add x1, other arithmetic, body(): jax.ops.segment_sum(arrived.reshape(-1, emb_width), arrived_rows.reshape(...  23.2 us
    scatter-add x1, other arithmetic, body(): jax.ops.segment_sum(dpooled.reshape(batch * features, emb_width), index.r...  23.2 us
    all_to_all x3, starting transfers between devices, from_everyone(): lax.all_to_all(jnp.broadcast_to(shard[None], (length, *shard.shape)), axi...  19.3 us
    all_to_all x1, waiting for transfers between devices, in_one_piece(): lax.all_to_all(both, axis, split_axis=split_dim, concat_axis=concat_dim,...  19.3 us
    unnamed x30, local copies, waits for them, and re-layouts  14 us
  transfers between devices with their start and end apart: 7, of which 5 were waited for; matrix products, arithmetic and copies ran while one was open for 26% of the time, Pallas kernels for 0%

commit v1 on v0

v1 whole, which is shorter than its diff:
```python
import functools

import jax
import jax.numpy as jnp
from jax import lax
from jax.experimental import pallas as pl
from jax.experimental.pallas import tpu as pltpu
from jax.sharding import Mesh
from jax.sharding import PartitionSpec as P

DP = ("dp_0", "dp_1", "dp_2")
DP_MP = ("dp_0", "dp_1", "dp_2", "mp")

clip_norm = 1.0
dense_rate = 0.02
table_rate = 0.5
adagrad_eps = 1e-10

F32 = jnp.float32
BF16 = jnp.bfloat16
I32 = jnp.int32
MESH = pl.DeviceIdType.MESH
VM = pl.BlockSpec(memory_space=pltpu.VMEM)
ANY = pl.BlockSpec(memory_space=pl.ANY)


def mm(a, b, ca, cb):
    return lax.dot_general(a, b, (((ca,), (cb,)), ((), ())), preferred_element_type=F32)


def iota(shape, dim):
    return lax.broadcasted_iota(I32, shape, dim)


def position():
    return tuple(lax.axis_index(a) for a in DP_MP)


def place(index):
    return {
        "dp_0": index // 32,
        "dp_1": (index // 8) % 4,
        "dp_2": (index // 4) % 2,
        "mp": index % 4,
    }


class Copies:
    def __init__(self, send, recv):
        self.send, self.recv, self.used, self.open = send, recv, 0, []

    def go(self, src, dst, where):
        k = self.used
        self.used += 1
        copy = pltpu.make_async_remote_copy(
            src_ref=src,
            dst_ref=dst,
            send_sem=self.send.at[k],
            recv_sem=self.recv.at[k],
            device_id=where,
            device_id_type=MESH,
        )
        copy.start()
        self.open.append(copy)
        return copy

    def drain(self):
        for copy in self.open:
            copy.wait_send()


def owner_bounds(counts_ref):
    counts = jnp.broadcast_to(counts_ref[...].astype(F32), (128, 128))
    upto = jnp.where(iota((128, 128), 0) <= iota((128, 128), 1), 1.0, 0.0).astype(BF16)
    ends = mm(counts.astype(BF16), upto, 1, 0)
    return (ends - counts).T, ends.T


def slot_rows(lookups, starts, ends):
    q = lookups.astype(F32)
    outs = []
    for part in range(q.shape[1] // 128):
        row = q[:, part * 128 : part * 128 + 128]
        hit = (row >= starts) & (row < ends)
        owner = iota((128, 128), 0).astype(F32)
        shift = jnp.sum(jnp.where(hit, owner * 32.0 - starts, 0.0), axis=0, keepdims=True)
        outs.append(row + shift)
    return jnp.concatenate(outs, axis=1)


def as_column(row):
    parts = []
    for part in range(row.shape[1] // 128):
        piece = row[:, part * 128 : part * 128 + 128]
        parts.append(jnp.broadcast_to(piece, (128, 128)).T)
    return jnp.concatenate(parts, axis=0)


def gather_kernel(lookups_ref, counts_ref, slab_ref, out_ref):
    starts, ends = owner_bounds(counts_ref)
    batch = lookups_ref.shape[1]

    def pair(k, carry):
        lane = iota((batch, 128), 1)
        got = []
        for side in range(2):
            slot = slot_rows(lookups_ref[pl.ds(2 * k + side, 1), :], starts, ends)
            column = as_column(slot).astype(I32)
            half, odd = column // 2, column % 2
            hot = jnp.concatenate(
                [
                    jnp.where(half == lane + 128 * t, 1.0, 0.0).astype(BF16)
                    for t in range(slab_ref.shape[0] // 128)
                ],
                axis=1,
            )
            both = mm(hot, slab_ref[...], 1, 0)
            one = jnp.where((lane >= 64) == (odd == 1), both, 0.0)
            got.append(one + pltpu.roll(one, 64, 1))
        out = jnp.where(lane < 64, got[0], got[1]).astype(BF16)
        out_ref[:, pl.ds(pl.multiple_of(k * 128, 128), 128)] = out
        return carry

    lax.fori_loop(0, lookups_ref.shape[0] // 2, pair, 0)


def segment_kernel(lookups_ref, counts_ref, grad_ref, out_ref, square_ref, acc):
    starts, ends = owner_bounds(counts_ref)
    batch = lookups_ref.shape[1]
    pairs = acc.shape[0]
    acc[...] = jnp.zeros_like(acc)

    def pair(k, carry):
        lane = iota((batch, 128), 1)
        block = grad_ref[:, pl.ds(pl.multiple_of(k * 128, 128), 128)]
        turned = pltpu.roll(block, 64, 1)
        hots, rows = [], []
        for side in range(2):
            slot = slot_rows(lookups_ref[pl.ds(2 * k + side, 1), :], starts, ends).astype(I32)
            hots.append(
                jnp.where(iota((pairs, batch), 0) == slot // 2, 1.0, 0.0).astype(BF16)
            )
            odd = as_column((slot % 2).astype(F32))
            same = jnp.where((lane < 64) == (side == 0), block, turned)
            kept = jnp.where((lane >= 64) == (odd > 0.5), same, 0.0)
            high = kept.astype(BF16)
            low = (kept - high.astype(F32)).astype(BF16)
            rows.append(jnp.concatenate([high, low], axis=1))
        acc[...] += mm(
            jnp.concatenate(hots, axis=1), jnp.concatenate(rows, axis=0), 1, 0
        )
        return carry

    lax.fori_loop(0, lookups_ref.shape[0] // 2, pair, 0)
    total = acc[:, :128] + acc[:, 128:]
    out_ref[...] = total.astype(BF16)
    square_ref[...] = jnp.sum((total * total).reshape(pairs // 8, 8, 128), axis=0)


def table_kernel(
    arrived_ref, even_ref, odd_ref, scale_ref, table_ref, accum_ref, new_ref, accum_new_ref, acc
):
    pairs = acc.shape[0]
    rows = 2 * pairs
    acc[...] = jnp.zeros_like(acc)
    step = 256

    def part(t, carry):
        lane = iota((step, 128), 1)
        base = pl.multiple_of(t * step, step)
        block = arrived_ref[pl.ds(base, step), :].astype(F32)
        turned = pltpu.roll(block, 64, 1)
        hots, values = [], []
        for side, ids_ref in enumerate((even_ref, odd_ref)):
            ids = jnp.concatenate(
                [ids_ref[pl.ds(2 * t, 1), :], ids_ref[pl.ds(2 * t + 1, 1), :]], axis=1
            )
            upper = ids >= pairs
            hots.append(
                jnp.where(
                    iota((pairs, step), 0) == jnp.where(upper, ids - pairs, ids), 1.0, 0.0
                ).astype(BF16)
            )
            high = as_column(jnp.where(upper, 1.0, 0.0))
            same = jnp.where((lane < 64) == (side == 0), block, turned)
            values.append(jnp.where((lane >= 64) == (high > 0.5), same, 0.0).astype(BF16))
        acc[...] += mm(
            jnp.concatenate(hots, axis=1), jnp.concatenate(values, axis=0), 1, 0
        )
        return carry

    lax.fori_loop(0, arrived_ref.shape[0] // step, part, 0)
    scale = scale_ref[0:1, 0:1]
    for p in range(pairs // 128):
        both = acc[128 * p : 128 * p + 128, :].T * scale
        for upper in range(2):
            r = both[64 * upper : 64 * upper + 64, :]
            line = p + upper * (pairs // 128)
            fresh = accum_ref[line : line + 1, :] + jnp.sum(r * r, axis=0, keepdims=True) / 64.0
            accum_new_ref[line : line + 1, :] = fresh
            at = line * 128
            new_ref[:, at : at + 128] = table_ref[:, at : at + 128] - table_rate * r / (
                jnp.sqrt(fresh) + adagrad_eps
            )


N_MAIN = 64


def main_kernel(
    pooled_ref, w_ref, bias_ref, wout_ref, label_ref, sw_ref, ids_ref,
    grad_ref, dp_ref, sq_ref, rids_ref,
    G, fac, hidden, dact, pacc, lg, LR, DL, gb, go, sv, rv,
    ZS, Df, ZRL, ZRR, ZL, ZR,
    GP, R0, SB, RL, RV, Q, RL2, RV2,
    ssem, rsem, bulk,
):
    x, y, c, z = position()
    dp = (x * 4 + y) * 2 + c
    me = dp * 4 + z
    cp = Copies(ssem, rsem)
    go_to = cp.go
    zr, zl, zo = (z + 1) % 4, (z + 3) % 4, (z + 2) % 4

    def send_ids(i, carry):
        p = (me + i) % 128
        pltpu.make_async_remote_copy(
            src_ref=ids_ref.at[p], dst_ref=rids_ref.at[me], send_sem=bulk.at[0],
            recv_sem=bulk.at[1], device_id=place(p), device_id_type=MESH,
        ).start()
        return carry

    a1 = go_to(pooled_ref.at[0:128], G.at[pl.ds(z * 256, 128)], {"mp": zr})
    b1 = go_to(pooled_ref.at[128:256], G.at[pl.ds(z * 256 + 128, 128)], {"mp": zl})
    a2 = go_to(pooled_ref.at[128:256], G.at[pl.ds(z * 256 + 128, 128)], {"mp": zr})
    b2 = go_to(pooled_ref.at[0:128], G.at[pl.ds(z * 256, 128)], {"mp": zl})
    lax.fori_loop(1, 128, send_ids, 0)
    rids_ref[me] = ids_ref[me]
    G[pl.ds(z * 256, 256), :] = pooled_ref[...]

    def forward(src):
        rows = pl.ds(pl.multiple_of(src * 256, 256), 256)
        pacc[...] = jnp.zeros_like(pacc)

        def tile(t, carry):
            cols = pl.ds(pl.multiple_of(t * 512, 512), 512)
            a = mm(G[rows, :], w_ref[:, cols], 1, 0) + bias_ref[:, cols]
            wo = wout_ref[:, cols]
            sg = lax.logistic(a)
            h = (a * sg).astype(BF16)
            hidden[rows, cols] = h
            fac[rows, cols] = wo * sg * (1.0 + a * (1.0 - sg))
            m = h.astype(F32) * wo
            pacc[...] += (m[:, 0:128] + m[:, 128:256]) + (m[:, 256:384] + m[:, 384:512])
            return carry

        lax.fori_loop(0, 4, tile, 0)
        for s in range(2):
            line = jnp.sum(pacc[128 * s : 128 * s + 128, :].T, axis=0, keepdims=True)
            lg[pl.ds(src * 2 + s, 1), :] = line

    forward(z)
    a1.wait_recv()
    a3 = go_to(
        G.at[pl.ds(zl * 256, 128)], G.at[pl.ds(zl * 256, 128)], {"mp": zr}
    )
    b1.wait_recv()
    b3 = go_to(
        G.at[pl.ds(zr * 256 + 128, 128)], G.at[pl.ds(zr * 256 + 128, 128)], {"mp": zl}
    )
    a2.wait_recv()
    forward(zl)
    b2.wait_recv()
    forward(zr)
    a3.wait_recv()
    b3.wait_recv()
    forward(zo)

    sent = [go_to(lg, LR.at[z], {"mp": (z + d) % 4}) for d in (1, 2, 3)]
    LR[z] = lg[...]
    for copy in sent:
        copy.wait_recv()
    logit = (LR[0] + LR[1]) + (LR[2] + LR[3])
    DL[...] = sw_ref[...] * (lax.logistic(logit) - label_ref[...])

    gb[...] = jnp.zeros_like(gb)
    go[...] = jnp.zeros_like(go)

    def dact_part(g, carry):
        rows = pl.ds(pl.multiple_of(g * 128, 128), 128)
        col = jnp.broadcast_to(DL[pl.ds(g, 1), :], (128, 128)).T
        for t in range(16):
            cols = slice(128 * t, 128 * t + 128)
            d = (fac[rows, cols] * col).astype(BF16)
            dact[rows, cols] = d
            gb[:, cols] += jnp.sum(d.astype(F32).reshape(16, 8, 128), axis=0)
            m = hidden[rows, cols].astype(F32) * col
            go[:, cols] += jnp.sum(m.reshape(16, 8, 128), axis=0)
        return carry

    lax.fori_loop(0, 8, dact_part, 0)
    for t in range(16):
        cols = slice(128 * t, 128 * t + 128)
        sv[t] = jnp.sum(gb[:, cols], axis=0, keepdims=True)
        sv[16 + t] = jnp.sum(go[:, cols], axis=0, keepdims=True)

    def send_small(i, carry):
        p = (dp + i) % 32
        where = {"dp_0": p // 8, "dp_1": (p // 2) % 4, "dp_2": p % 2, "mp": z}
        pltpu.make_async_remote_copy(
            src_ref=sv.at[p], dst_ref=rv.at[dp], send_sem=bulk.at[2],
            recv_sem=bulk.at[3], device_id=where, device_id_type=MESH,
        ).start()
        return carry

    lax.fori_loop(1, 32, send_small, 0)
    rv[dp] = sv[dp]

    def dpool(dest, put):
        rows = pl.ds(pl.multiple_of(dest * 256, 256), 256)

        def tile(t, carry):
            at = pl.multiple_of(t * 512, 512)
            put(mm(dact[rows, :], w_ref[pl.ds(at, 512), :], 1, 1), pl.ds(at, 512))
            return carry

        lax.fori_loop(0, 2, tile, 0)

    def put_far(d, cols):
        ZS[0, :, cols] = d.astype(BF16)

    dpool(zo, put_far)
    z1 = go_to(ZS.at[0, 0:128], ZRL, {"mp": zr})
    z2 = go_to(ZS.at[0, 128:256], ZRR, {"mp": zl})

    def put_right(d, cols):
        Df[0, :, cols] = d[0:128]
        ZS[1, 128:256, cols] = d[128:256].astype(BF16)

    dpool(zr, put_right)
    z3 = go_to(ZS.at[1, 128:256], ZL.at[128:256], {"mp": zr})

    def put_left(d, cols):
        ZS[2, 0:128, cols] = d[0:128].astype(BF16)
        Df[1, :, cols] = d[128:256]

    dpool(zl, put_left)
    z4 = go_to(ZS.at[2, 0:128], ZR.at[0:128], {"mp": zl})

    partner = {"dp_2": 1 - c}
    to_core = {}

    def weight_grad(xi, tag):
        at = pl.multiple_of(xi * 256, 256)

        def tile(t, carry):
            cols = pl.ds(pl.multiple_of(t * 512, 512), 512)
            g = mm(G[:, pl.ds(at, 256)], dact[:, cols], 0, 0)
            for yi in range(4):
                for ci in range(2):
                    r = (yi * 2 + ci) * 32
                    GP[xi, yi, ci, :, cols] = g[r : r + 32]
            return carry

        lax.fori_loop(0, 4, tile, 0)
        to_core[tag] = go_to(GP.at[xi, :, 1 - c], R0.at[xi], partner)

    def chip_sum(xi, tag):
        to_core[tag].wait_recv()
        for yi in range(4):
            s = R0[xi, yi] + GP[xi, yi, c]
            R0[xi, yi] = s
            SB[xi, yi] = s.astype(BF16)

    xr, xl, xo = (x + 1) % 4, (x + 3) % 4, (x + 2) % 4
    yr, yl, yo = (y + 1) % 4, (y + 3) % 4, (y + 2) % 4
    LO, HI = slice(0, 1024), slice(1024, 2048)

    weight_grad(xo, "o")
    weight_grad(xr, "r")
    z1.wait_recv()
    ZS[1, 0:128, :] = (Df[0] + ZRL[...].astype(F32)).astype(BF16)
    z5 = go_to(ZS.at[1, 0:128], ZL.at[0:128], {"mp": zr})
    z2.wait_recv()
    ZS[2, 128:256, :] = (Df[1] + ZRR[...].astype(F32)).astype(BF16)
    z6 = go_to(ZS.at[2, 128:256], ZR.at[128:256], {"mp": zl})
    chip_sum(xo, "o")
    h0a = go_to(SB.at[xo, 0:2, :, LO], RL.at[0, 0], {"dp_0": xr})
    h0b = go_to(SB.at[xo, 2:4, :, LO], RL.at[0, 1], {"dp_0": xl})
    weight_grad(xl, "l")
    chip_sum(xr, "r")
    h0c = go_to(SB.at[xr, 2:4, :, LO], RV.at[0, 0, 2:4], {"dp_0": xr})
    weight_grad(x, "m")
    chip_sum(xl, "l")
    h0d = go_to(SB.at[xl, 0:2, :, LO], RV.at[0, 1, 0:2], {"dp_0": xl})
    chip_sum(x, "m")
    h1a = go_to(SB.at[0:2, yo, :, HI], RL.at[1, 0], {"dp_1": yr})
    h1b = go_to(SB.at[2:4, yo, :, HI], RL.at[1, 1], {"dp_1": yl})
    h1c = go_to(SB.at[2:4, yr, :, HI], RV.at[1, 0, 2:4], {"dp_1": yr})
    h1d = go_to(SB.at[0:2, yl, :, HI], RV.at[1, 1, 0:2], {"dp_1": yl})

    def put_own(d, cols):
        dp_ref[:, cols] = d

    dpool(z, put_own)

    h0a.wait_recv()
    for k in range(2):
        SB[xr, k, :, LO] = (R0[xr, k, :, LO] + RL[0, 0, k].astype(F32)).astype(BF16)
    h0e = go_to(SB.at[xr, 0:2, :, LO], RV.at[0, 0, 0:2], {"dp_0": xr})
    h0b.wait_recv()
    for k in range(2):
        SB[xl, 2 + k, :, LO] = (R0[xl, 2 + k, :, LO] + RL[0, 1, k].astype(F32)).astype(BF16)
    h0f = go_to(SB.at[xl, 2:4, :, LO], RV.at[0, 1, 2:4], {"dp_0": xl})
    h1a.wait_recv()
    for k in range(2):
        SB[k, yr, :, HI] = (R0[k, yr, :, HI] + RL[1, 0, k].astype(F32)).astype(BF16)
    h1e = go_to(SB.at[0:2, yr, :, HI], RV.at[1, 0, 0:2], {"dp_1": yr})
    h1b.wait_recv()
    for k in range(2):
        SB[2 + k, yl, :, HI] = (R0[2 + k, yl, :, HI] + RL[1, 1, k].astype(F32)).astype(BF16)
    h1f = go_to(SB.at[2:4, yl, :, HI], RV.at[1, 1, 2:4], {"dp_1": yl})

    def second(h, axis, n):
        nr, nl, no = (n + 1) % 4, (n + 3) % 4, (n + 2) % 4
        s1 = go_to(Q.at[h, no, 0:16], RL2.at[h, 0], {axis: nr})
        s2 = go_to(Q.at[h, no, 16:32], RL2.at[h, 1], {axis: nl})
        s3 = go_to(Q.at[h, nr, 16:32], RV2.at[h, 0, 16:32], {axis: nr})
        s4 = go_to(Q.at[h, nl, 0:16], RV2.at[h, 1, 0:16], {axis: nl})
        return nr, nl, (s1, s2, s3, s4)

    def second_relay(h, axis, state):
        nr, nl, (s1, s2, s3, s4) = state
        s1.wait_recv()
        Q[h, nr, 0:16] = Q[h, nr, 0:16] + RL2[h, 0]
        s5 = go_to(Q.at[h, nr, 0:16], RV2.at[h, 0, 0:16], {axis: nr})
        s2.wait_recv()
        Q[h, nl, 16:32] = Q[h, nl, 16:32] + RL2[h, 1]
        s6 = go_to(Q.at[h, nl, 16:32], RV2.at[h, 1, 16:32], {axis: nl})
        return s3, s4, s5, s6

    for copy in (h0c, h0d, h0e, h0f):
        copy.wait_recv()
    for k in range(4):
        Q[0, k] = R0[x, k, :, LO] + (RV[0, 0, k].astype(F32) + RV[0, 1, k].astype(F32))
    t0 = second(0, "dp_1", y)
    for copy in (h1c, h1d, h1e, h1f):
        copy.wait_recv()
    for k in range(4):
        Q[1, k] = R0[k, y, :, HI] + (RV[1, 0, k].astype(F32) + RV[1, 1, k].astype(F32))
    t1 = second(1, "dp_0", x)
    u0 = second_relay(0, "dp_1", t0)
    u1 = second_relay(1, "dp_0", t1)

    for copy in (z3, z4, z5, z6):
        copy.wait_recv()
    dp_ref[...] = dp_ref[...] + (ZL[...].astype(F32) + ZR[...].astype(F32))

    small = sv.at[pl.ds(0, 31)]
    pltpu.make_async_copy(small, small, bulk.at[2]).wait()
    pltpu.make_async_copy(small, small, bulk.at[3]).wait()
    few = jnp.sum(rv[...], axis=0)
    few = jnp.where(iota((8, 128), 0) == 0, jnp.broadcast_to(few * few, (8, 128)), 0.0)

    for copy in u0 + u1:
        copy.wait_recv()
    left = Q[0, y] + (RV2[0, 0] + RV2[0, 1])
    right = Q[1, x] + (RV2[1, 0] + RV2[1, 1])
    grad_ref[:, LO] = left
    grad_ref[:, HI] = right
    both = left * left + right * right
    both = jnp.sum(both.reshape(4, 8, 1024), axis=0)
    for t in range(8):
        few = few + both[:, 128 * t : 128 * t + 128]
    sq_ref[...] = few

    lot = ids_ref.at[pl.ds(0, 127)]
    pltpu.make_async_copy(lot, lot, bulk.at[0]).wait()
    pltpu.make_async_copy(lot, lot, bulk.at[1]).wait()
    cp.drain()


N_XCHG = 40


def exchange_kernel(
    slot_ref, sqa_ref, sqb_ref, grad_ref, accum_ref, w_ref,
    wn_ref, accum_new_ref, arrived_ref, scale_ref,
    ns, NR, wpart, ssem, rsem, bulk, local,
):
    x, y, c, z = position()
    dp = (x * 4 + y) * 2 + c
    me = dp * 4 + z
    cp = Copies(ssem, rsem)
    go_to = cp.go
    fetch = pltpu.make_async_copy(w_ref.at[pl.ds(dp * 32, 32)], wpart, local)
    fetch.start()
    ns[...] = jnp.sum(sqa_ref[...] + sqb_ref[...], axis=0, keepdims=True)

    def send_norm(i, carry):
        p = (me + i) % 128
        pltpu.make_async_remote_copy(
            src_ref=ns, dst_ref=NR.at[me], send_sem=bulk.at[0],
            recv_sem=bulk.at[1], device_id=place(p), device_id_type=MESH,
        ).start()
        return carry

    def send_slots(i, carry):
        p = (me + i) % 128
        pltpu.make_async_remote_copy(
            src_ref=slot_ref.at[p], dst_ref=arrived_ref.at[me], send_sem=bulk.at[2],
            recv_sem=bulk.at[3], device_id=place(p), device_id_type=MESH,
        ).start()
        return carry

    lax.fori_loop(1, 128, send_norm, 0)
    lax.fori_loop(1, 128, send_slots, 0)
    NR[me] = ns[...]
    arrived_ref[me] = slot_ref[me]

    lot = NR.at[pl.ds(0, 127)]
    pltpu.make_async_copy(lot, lot, bulk.at[1]).wait()
    lanes = jnp.sum(NR[...], axis=0)
    total = jnp.sum(lanes, axis=1, keepdims=True)
    scale = clip_norm / jnp.maximum(jnp.sqrt(total), clip_norm)
    scale_ref[...] = jnp.broadcast_to(scale, (8, 128))
    fetch.wait()
    clipped = scale * grad_ref[...]
    fresh = accum_ref[...] + clipped * clipped
    accum_new_ref[...] = fresh
    wn_ref[x, y, c] = (
        wpart[...].astype(F32) - dense_rate * clipped / (jnp.sqrt(fresh) + adagrad_eps)
    ).astype(BF16)

    xr, xl, xo = (x + 1) % 4, (x + 3) % 4, (x + 2) % 4
    yr, yl, yo = (y + 1) % 4, (y + 3) % 4, (y + 2) % 4
    LO, HI = slice(0, 1024), slice(1024, 2048)
    T, B = slice(0, 16), slice(16, 32)
    partner = {"dp_2": 1 - c}

    def same(ref, where):
        return go_to(ref, ref, where)

    p1 = same(wn_ref.at[x, y, c, :, LO], {"dp_0": xr})
    p2 = same(wn_ref.at[x, y, c, :, LO], {"dp_0": xl})
    q1 = same(wn_ref.at[x, y, c, :, HI], {"dp_1": yr})
    q2 = same(wn_ref.at[x, y, c, :, HI], {"dp_1": yl})
    p1.wait_recv()
    p3 = same(wn_ref.at[xl, y, c, T, LO], {"dp_0": xr})
    p2.wait_recv()
    p4 = same(wn_ref.at[xr, y, c, B, LO], {"dp_0": xl})
    q1.wait_recv()
    q3 = same(wn_ref.at[x, yl, c, T, HI], {"dp_1": yr})
    q2.wait_recv()
    q4 = same(wn_ref.at[x, yr, c, B, HI], {"dp_1": yl})
    p3.wait_recv()
    p4.wait_recv()
    p5 = same(wn_ref.at[:, y, c, :, LO], {"dp_1": yr})
    p6 = same(wn_ref.at[:, y, c, :, LO], {"dp_1": yl})
    q3.wait_recv()
    q4.wait_recv()
    q5 = same(wn_ref.at[x, :, c, :, HI], {"dp_0": xr})
    q6 = same(wn_ref.at[x, :, c, :, HI], {"dp_0": xl})
    d = [same(wn_ref.at[:, y, c, :, LO], partner), same(wn_ref.at[x, :, c, :, HI], partner)]
    p5.wait_recv()
    p7 = same(wn_ref.at[0:2, yl, c, :, LO], {"dp_1": yr})
    p6.wait_recv()
    p8 = same(wn_ref.at[2:4, yr, c, :, LO], {"dp_1": yl})
    q5.wait_recv()
    q7 = same(wn_ref.at[xl, 0:2, c, :, HI], {"dp_0": xr})
    q6.wait_recv()
    q8 = same(wn_ref.at[xr, 2:4, c, :, HI], {"dp_0": xl})
    d += [same(wn_ref.at[:, yl, c, :, LO], partner), same(wn_ref.at[:, yr, c, :, LO], partner)]
    d += [same(wn_ref.at[xl, :, c, :, HI], partner), same(wn_ref.at[xr, :, c, :, HI], partner)]
    for copy in (p7, p8, q7, q8):
        copy.wait_recv()
    d += [same(wn_ref.at[:, yo, c, :, LO], partner), same(wn_ref.at[xo, :, c, :, HI], partner)]
    for copy in d:
        copy.wait_recv()
    pltpu.make_async_copy(lot, lot, bulk.at[0]).wait()
    many = arrived_ref.at[pl.ds(0, 127)]
    pltpu.make_async_copy(many, many, bulk.at[2]).wait()
    pltpu.make_async_copy(many, many, bulk.at[3]).wait()
    cp.drain()


def shape(dims, kind):
    return jax.ShapeDtypeStruct(dims, kind)


def gather_pooled(lookups, counts, slab):
    return pl.pallas_call(
        gather_kernel,
        out_shape=shape((256, 1024), BF16),
        in_specs=[VM] * 3,
        out_specs=VM,
        name="gather_pooled",
    )(lookups, counts, slab)


def segment_slots(lookups, counts, dpooled):
    return pl.pallas_call(
        segment_kernel,
        out_shape=(shape((2048, 128), BF16), shape((8, 128), F32)),
        in_specs=[VM] * 3,
        out_specs=(VM, VM),
        scratch_shapes=[pltpu.VMEM((2048, 256), F32)],
        name="segment_slots",
    )(lookups, counts, dpooled)


def table_update(arrived, even, odd, scale, table, accum):
    return pl.pallas_call(
        table_kernel,
        out_shape=(shape((64, 4096), F32), shape((32, 128), F32)),
        in_specs=[VM] * 6,
        out_specs=(VM, VM),
        scratch_shapes=[pltpu.VMEM((2048, 128), F32)],
        name="table_update",
    )(arrived, even, odd, scale, table, accum)


def tower(pooled, w, bias, wout, labels, sw, ids):
    V = pltpu.VMEM
    return pl.pallas_call(
        main_kernel,
        out_shape=(
            shape((32, 2048), F32),
            shape((256, 1024), F32),
            shape((8, 128), F32),
            shape((128, 1, 128), I32),
        ),
        in_specs=[VM] * 7,
        out_specs=(VM,) * 4,
        scratch_shapes=[
            V((1024, 1024), BF16), V((1024, 2048), F32), V((1024, 2048), BF16),
            V((1024, 2048), BF16), V((256, 128), F32), V((8, 128), F32), V((4, 8, 128), F32),
            V((8, 128), F32), V((8, 2048), F32), V((8, 2048), F32),
            V((32, 1, 128), F32), V((32, 1, 128), F32),
            V((3, 256, 1024), BF16), V((2, 128, 1024), F32),
            V((128, 1024), BF16), V((128, 1024), BF16),
            V((256, 1024), BF16), V((256, 1024), BF16),
            V((4, 4, 2, 32, 2048), F32), V((4, 4, 32, 2048), F32), V((4, 4, 32, 2048), BF16),
            V((2, 2, 2, 32, 1024), BF16), V((2, 2, 4, 32, 1024), BF16),
            V((2, 4, 32, 1024), F32), V((2, 2, 16, 1024), F32), V((2, 2, 32, 1024), F32),
            pltpu.SemaphoreType.DMA((N_MAIN,)), pltpu.SemaphoreType.DMA((N_MAIN,)),
            pltpu.SemaphoreType.DMA((4,)),
        ],
        compiler_params=pltpu.CompilerParams(
            has_side_effects=True, vmem_limit_bytes=62 * 1024 * 1024
        ),
        name="tower",
    )(pooled, w, bias, wout, labels, sw, ids)


def exchange(slots, sqa, sqb, grad, accum, w):
    V = pltpu.VMEM
    return pl.pallas_call(
        exchange_kernel,
        out_shape=(
            shape((4, 4, 2, 32, 2048), BF16),
            shape((32, 2048), F32),
            shape((128, 16, 128), BF16),
            shape((8, 128), F32),
        ),
        in_specs=[VM] * 5 + [ANY],
        out_specs=(VM,) * 4,
        scratch_shapes=[
            V((1, 128), F32), V((128, 1, 128), F32), V((32, 2048), BF16),
            pltpu.SemaphoreType.DMA((N_XCHG,)), pltpu.SemaphoreType.DMA((N_XCHG,)),
            pltpu.SemaphoreType.DMA((4,)), pltpu.SemaphoreType.DMA,
        ],
        compiler_params=pltpu.CompilerParams(has_side_effects=True),
        name="exchange",
    )(slots, sqa, sqb, grad, accum, w)


def body(
    slab_values,
    row_ids,
    peer_counts,
    lookup_slots,
    labels,
    sample_weight,
    weight_in,
    bias_in,
    weight_out,
    dense_accum,
    table_rows,
    table_accum,
):
    lookups = lookup_slots.T
    slab = slab_values[0].reshape(2048, 128)
    ids = row_ids[0]
    ids = jnp.concatenate([ids[:, 0::2], ids[:, 1::2]], axis=1)
    ids = jnp.pad(ids, ((0, 0), (0, 96))).reshape(128, 1, 128)
    pooled = gather_pooled(lookups, peer_counts, slab)
    grad, dpooled, dense_sq, got = tower(
        pooled,
        weight_in,
        bias_in.reshape(1, 2048),
        weight_out.astype(F32).reshape(1, 2048),
        labels.astype(F32).reshape(8, 128),
        sample_weight.reshape(8, 128),
        ids,
    )
    slots, slot_sq = segment_slots(lookups, peer_counts, dpooled)
    wn, accum_new, arrived, scale = exchange(
        slots.reshape(128, 16, 128), dense_sq, slot_sq, grad, dense_accum, weight_in
    )
    even = got[:, 0, 0:16].reshape(16, 128)
    odd = got[:, 0, 16:32].reshape(16, 128)
    table_new, table_accum_new = table_update(
        arrived.reshape(2048, 128), even, odd, scale, table_rows.T,
        table_accum.reshape(32, 128),
    )
    return (
        wn.reshape(1024, 2048), accum_new, table_new.T, table_accum_new.reshape(4096)
    )


def solution(mesh):
    torus = Mesh(mesh.devices.reshape(4, 4, 2, mesh.shape["mp"]), ("dp_0", "dp_1", "dp_2", "mp"))
    placed = (
        P(DP_MP, None, None),
        P(DP_MP, None, None),
        P(DP_MP, None),
        P(DP_MP, None),
        P(DP),
        P(DP),
        P(None, "mp"),
        P("mp"),
        P("mp"),
        P(DP, "mp"),
        P(DP_MP, None),
        P(DP_MP),
    )
    return jax.shard_map(
        body,
        mesh=torus,
        in_specs=placed,
        out_specs=(P(None, "mp"), P(DP, "mp"), P(DP_MP, None), P(DP_MP)),
        check_vma=False,
    )
```

time: 329 us -> 173 us (0.53)
  Pallas kernels: 0 us -> 157 us
  waiting for transfers between devices: 96.5 us -> 0 us
  other arithmetic: 77.7 us -> 2.58 us
  blocking collectives: 31.6 us -> 0 us
  matrix products: 30.9 us -> 0 us
  starting transfers between devices: 30.5 us -> 0 us
  local copies, waits for them, and re-layouts: 42.7 us -> 12.5 us
  between operations: 17.7 us -> 0.66 us
    pallas_call x0 -> x5, Pallas kernels: none -> 157 us  [the longest x1 83.1 us: tower(): pl.pallas_call(main_kernel, out_shape=(shape((32, 2048), F32), shape((256...]
    all_to_all x5 -> x0, waiting for transfers between devices: 96.4 us -> none  [the longest x1 46.6 us: sum_at_owner(): lax.all_to_all(pieces, axis, split_axis=0, concat_axis=0, tiled=True)]
    scatter-add x2 -> x0, other arithmetic: 46.4 us -> none  [the longest x1 23.2 us: body(): jax.ops.segment_sum(arrived.reshape(-1, emb_width), arrived_rows.reshape(...]
    psum x4 -> x0, blocking collectives: 31.6 us -> none  [over_axes(): return functools.reduce(lax.psum, axes, shard)]
    dot_general x5 -> x0, matrix products: 30.9 us -> none  [the longest x1 10.4 us: body(): lax.dot_general(dact, weight_in, (((1,), (1,)), ((), ())), preferred_elem...]
    all_to_all x5 -> x0, starting transfers between devices: 30.1 us -> none  [the longest x3 19.3 us: from_everyone(): lax.all_to_all(jnp.broadcast_to(shard[None], (length, *shard.shape)), axi...]
    reduce_sum x10 -> x0, other arithmetic: 24.7 us -> none  [the longest x1 5.96 us: body(): grad_bias = jnp.sum(dact.astype(jnp.float32), axis=0)]
    gather x1 -> x0, local copies, waits for them, and re-layouts: 12.1 us -> none  [body(): pooled = slab_view[index].reshape(batch, features * emb_width)]
  transfers between devices with their start and end apart: 7 -> 0, of which waited for: 5 -> 0; matrix products, arithmetic and copies ran while one was open for 26% -> 0% of each run, Pallas kernels for 0% -> 0%
where the time goes in v1:
time: 173 us; the launch traced here: 172 us
  Pallas kernels  157 us (91%)
  local copies, waits for them, and re-layouts  12.5 us (7%)
  other arithmetic  2.58 us (1%)
    pallas_call x1, Pallas kernels, tower(): pl.pallas_call(main_kernel, out_shape=(shape((32, 2048), F32), shape((256...  83.1 us
    pallas_call x1, Pallas kernels, exchange(): pl.pallas_call(exchange_kernel, out_shape=(shape((4, 4, 2, 32, 2048), BF1...  43.2 us
    pallas_call x1, Pallas kernels, segment_slots(): pl.pallas_call(segment_kernel, out_shape=(shape((2048, 128), BF16), shape...  10.3 us
    pallas_call x1, Pallas kernels, gather_pooled(): pl.pallas_call(gather_kernel, out_shape=shape((256, 1024), BF16), in_spec...  10.2 us
    pallas_call x1, Pallas kernels, table_update(): pl.pallas_call(table_kernel, out_shape=(shape((64, 4096), F32), shape((32...  9.8 us
    unnamed x4, local copies, waits for them, and re-layouts  5.54 us

profile of v1, /device:TPU:1, one launch (start us, length us, event | category | flops | bytes accessed | tf_op | source)
XLA Modules:
  0.0 172.2 jit_solution(15321498932157379119)
XLA Ops:
  0.6 1.3 convert_bitcast_fusion.label_ref
  1.9 0.7 slice.13
  2.6 0.7 slice.12
  3.4 1.3 reshape.51
  4.6 0.1 copy.18
  4.7 0.6 pad.4
  5.4 2.1 %reshape_squeeze.9.slab_ref = bf16[2048,128]{1,0:T(8,128)(2,1)} reshape(bf16[1,128,2048]{2,1,0:T(8,128)(2,1)} %param.12) | data formatting | bytes 1048576 | tf_op jit(solution)/shard_map/reshape;squeeze | solution.py:693
  7.5 10.2 %gather_pooled.1.pooled_ref = bf16[256,1024]{1,0:T(8,128)(2,1)} custom-call(s32[16,256]{1,0:T(8,128)} %bitcast.20, s32[1,128]{1,0:T(1,128)} %counts_ref.3, bf16[2048,128]{1,0:T(8,128)(2,1)} %reshape_squeeze.9.slab_ref), custom_call_target="tpu_custom_call" | custom-call | tf_op jit(solution)/shard_map/gather_pooled/pallas_call | solution.py:592
  17.6 83.1 %tower.1 = (f32[32,2048]{1,0:T(8,128)}, f32[256,1024]{1,0:T(8,128)}, f32[8,128]{1,0:T(8,128)}, s32[128,1,128]{2,1,0:T(1,128)}) custom-call(bf16[256,1024]{1,0:T(8,128)(2,1)} %gather_pooled.1.pooled_ref, bf16[1024,2048]{1,0:T(8,128)(2,1)} %w_ref.3, f32[1,2048]{1,0:T(1,128)} %bitcast.26, f32[1,2048]{1,0:T(1,128)} %bitcast.22, ...), custom_call_target="tpu_custom_call" | custom-call | tf_op jit(solution)/shard_map/tower/pallas_call | solution.py:625
  100.7 10.3 %segment_slots.1 = (bf16[2048,128]{1,0:T(8,128)(2,1)}, f32[8,128]{1,0:T(8,128)}) custom-call(s32[16,256]{1,0:T(8,128)} %bitcast.21, s32[1,128]{1,0:T(1,128)} %counts_ref.3, f32[256,1024]{1,0:T(8,128)} %get-tuple-element.16.grad_ref), custom_call_target="tpu_custom_call" | custom-call | tf_op jit(solution)/shard_map/segment_slots/pallas_call | solution.py:602
  111.0 1.3 slice_reduce_fusion
  112.4 0.7 reshape_squeeze.11.odd_ref
  113.0 0.7 reshape_squeeze.10.even_ref
  113.7 43.2 %exchange.1 = (bf16[4,4,2,32,2048]{4,3,2,1,0:T(8,128)(2,1)}, f32[32,2048]{1,0:T(8,128)}, bf16[128,16,128]{2,1,0:T(8,128)(2,1)}, f32[8,128]{1,0:T(8,128)}) custom-call(bf16[128,16,128]{2,1,0:T(8,128)(2,1)} %bitcast.17, f32[8,128]{1,0:T(8,128)} %get-tuple-element.18.sqa_ref, f32[8,128]{1,0:T(8,128)} %get-tuple-element.19.sqb_ref, ...), custom_call_target="tpu_custom_call" | custom-call | tf_op jit(solution)/shard_map/exchange/pallas_call | solution.py:658
  156.9 9.8 %table_update.1 = (f32[64,4096]{1,0:T(8,128)}, f32[32,128]{1,0:T(8,128)}) custom-call(bf16[2048,128]{1,0:T(8,128)(2,1)} %bitcast.18, s32[16,128]{1,0:T(8,128)} %reshape_squeeze.10.even_ref, s32[16,128]{1,0:T(8,128)} %reshape_squeeze.11.odd_ref, f32[8,128]{1,0:T(8,128)} %get-tuple-element.25.scale_ref, f32[64,4096]{1,0:T(8,128)} %bitcast.16, f32[32,128]{1,0:T(8,128)} %bitcast.23), custom_call_target="tpu_custom_call" | custom-call | tf_op jit(solution)/shard_map/table_update/pallas_call | solution.py:613
  166.7 0.0 copy-start
  166.7 4.8 %copy.21 = bf16[1024,2048]{1,0:T(8,128)(2,1)} copy(bf16[1024,2048]{1,0:T(8,128)(2,1)} %bitcast.15) | data formatting | bytes 8388608
  171.5 0.0 copy-done
  171.5 0.7 copy.22
  (1 shorter events, 0.0 us)
Async XLA Ops:
  166.7 4.8 %copy-start = (f32[32,2048]{1,0:T(8,128)S(1)}, f32[32,2048]{1,0:T(8,128)}, u32[]{:S(2)}) copy-start(f32[32,2048]{1,0:T(8,128)} %get-tuple-element.35) | copy-start | bytes 786436

commit v2 on v0

v2 whole, which is shorter than its diff:
```python
import functools

import jax
import jax.numpy as jnp
from jax import lax
from jax.experimental import pallas as pl
from jax.experimental.pallas import tpu as pltpu
from jax.sharding import Mesh
from jax.sharding import PartitionSpec as P

DP = ("dp_0", "dp_1", "dp_2")
DP_MP = ("dp_0", "dp_1", "dp_2", "mp")

clip_norm = 1.0
dense_rate = 0.02
table_rate = 0.5
adagrad_eps = 1e-10

F32 = jnp.float32
BF16 = jnp.bfloat16
I32 = jnp.int32
MESH = pl.DeviceIdType.MESH
VM = pl.BlockSpec(memory_space=pltpu.VMEM)
ANY = pl.BlockSpec(memory_space=pl.ANY)


def mm(a, b, ca, cb):
    return lax.dot_general(a, b, (((ca,), (cb,)), ((), ())), preferred_element_type=F32)


def iota(shape, dim):
    return lax.broadcasted_iota(I32, shape, dim)


def position():
    return tuple(lax.axis_index(a) for a in DP_MP)


def place(index):
    return {
        "dp_0": index // 32,
        "dp_1": (index // 8) % 4,
        "dp_2": (index // 4) % 2,
        "mp": index % 4,
    }


class Copies:
    def __init__(self, send, recv):
        self.send, self.recv, self.used, self.open = send, recv, 0, []

    def go(self, src, dst, where):
        k = self.used
        self.used += 1
        copy = pltpu.make_async_remote_copy(
            src_ref=src,
            dst_ref=dst,
            send_sem=self.send.at[k],
            recv_sem=self.recv.at[k],
            device_id=where,
            device_id_type=MESH,
        )
        copy.start()
        self.open.append(copy)
        return copy

    def drain(self):
        for copy in self.open:
            copy.wait_send()


def owner_bounds(counts_ref):
    counts = jnp.broadcast_to(counts_ref[...].astype(F32), (128, 128))
    upto = jnp.where(iota((128, 128), 0) <= iota((128, 128), 1), 1.0, 0.0).astype(BF16)
    ends = mm(counts.astype(BF16), upto, 1, 0)
    return (ends - counts).T, ends.T


def slot_rows(lookups, starts, ends):
    q = lookups.astype(F32)
    outs = []
    for part in range(q.shape[1] // 128):
        row = q[:, part * 128 : part * 128 + 128]
        hit = (row >= starts) & (row < ends)
        owner = iota((128, 128), 0).astype(F32)
        shift = jnp.sum(jnp.where(hit, owner * 32.0 - starts, 0.0), axis=0, keepdims=True)
        outs.append(row + shift)
    return jnp.concatenate(outs, axis=1)


def as_column(row):
    parts = []
    for part in range(row.shape[1] // 128):
        piece = row[:, part * 128 : part * 128 + 128]
        parts.append(jnp.broadcast_to(piece, (128, 128)).T)
    return jnp.concatenate(parts, axis=0)


def tiles_over_rows(index, count):
    high = jnp.floor(index * (1.0 / 16.0))
    low = index - 16.0 * high
    n = index.shape[1]
    inner = jnp.where(iota((16, n), 0).astype(F32) == low, 1.0, 0.0).astype(BF16)
    high = jnp.broadcast_to(high, (16, n)).astype(BF16)
    zero = jnp.zeros((16, n), BF16)
    return jnp.concatenate(
        [jnp.where(high == jnp.asarray(t, BF16), inner, zero) for t in range(count)], axis=0
    )


def tiles_over_lanes(column, count):
    high = jnp.floor(column * (1.0 / 128.0))
    low = column - 128.0 * high
    inner = jnp.where(iota(column.shape, 1).astype(F32) == low, 1.0, 0.0).astype(BF16)
    high = high.astype(BF16)
    zero = jnp.zeros(column.shape, BF16)
    return jnp.concatenate(
        [jnp.where(high == jnp.asarray(t, BF16), inner, zero) for t in range(count)], axis=1
    )


class Spread:
    LO, HI = slice(0, 1024), slice(1024, 2048)
    T, B = slice(0, 16), slice(16, 32)

    def __init__(self, ref, go, where):
        self.ref, self.go = ref, go
        self.x, self.y, self.c, _ = where
        self.xr, self.xl, self.xo = ((self.x + d) % 4 for d in (1, 3, 2))
        self.yr, self.yl, self.yo = ((self.y + d) % 4 for d in (1, 3, 2))
        self.partner = {"dp_2": 1 - self.c}
        self.d = []

    def same(self, piece, where):
        ref = self.ref.at[piece]
        return self.go(ref, ref, where)

    def first(self):
        x, y, c = self.x, self.y, self.c
        every = slice(None)
        self.p1 = self.same((x, y, c, every, self.LO), {"dp_0": self.xr})
        self.p2 = self.same((x, y, c, every, self.LO), {"dp_0": self.xl})
        self.q1 = self.same((x, y, c, every, self.HI), {"dp_1": self.yr})
        self.q2 = self.same((x, y, c, every, self.HI), {"dp_1": self.yl})

    def second(self):
        x, y, c = self.x, self.y, self.c
        self.p1.wait_recv()
        self.p3 = self.same((self.xl, y, c, self.T, self.LO), {"dp_0": self.xr})
        self.p2.wait_recv()
        self.p4 = self.same((self.xr, y, c, self.B, self.LO), {"dp_0": self.xl})
        self.q1.wait_recv()
        self.q3 = self.same((x, self.yl, c, self.T, self.HI), {"dp_1": self.yr})
        self.q2.wait_recv()
        self.q4 = self.same((x, self.yr, c, self.B, self.HI), {"dp_1": self.yl})

    def third(self):
        x, y, c = self.x, self.y, self.c
        every = slice(None)
        self.p3.wait_recv()
        self.p4.wait_recv()
        mine, other = (every, y, c, every, self.LO), (x, every, c, every, self.HI)
        self.p5 = self.same(mine, {"dp_1": self.yr})
        self.p6 = self.same(mine, {"dp_1": self.yl})
        self.q3.wait_recv()
        self.q4.wait_recv()
        self.q5 = self.same(other, {"dp_0": self.xr})
        self.q6 = self.same(other, {"dp_0": self.xl})
        self.d += [self.same(mine, self.partner), self.same(other, self.partner)]

    def fourth(self):
        c = self.c
        every = slice(None)
        self.p5.wait_recv()
        self.p7 = self.same((slice(0, 2), self.yl, c, every, self.LO), {"dp_1": self.yr})
        self.p6.wait_recv()
        self.p8 = self.same((slice(2, 4), self.yr, c, every, self.LO), {"dp_1": self.yl})
        self.q5.wait_recv()
        self.q7 = self.same((self.xl, slice(0, 2), c, every, self.HI), {"dp_0": self.xr})
        self.q6.wait_recv()
        self.q8 = self.same((self.xr, slice(2, 4), c, every, self.HI), {"dp_0": self.xl})
        for n in (self.yl, self.yr):
            self.d.append(self.same((every, n, c, every, self.LO), self.partner))
        for n in (self.xl, self.xr):
            self.d.append(self.same((n, every, c, every, self.HI), self.partner))

    def fifth(self):
        c = self.c
        every = slice(None)
        for copy in (self.p7, self.p8, self.q7, self.q8):
            copy.wait_recv()
        self.d.append(self.same((every, self.yo, c, every, self.LO), self.partner))
        self.d.append(self.same((self.xo, every, c, every, self.HI), self.partner))

    def last(self):
        for copy in self.d:
            copy.wait_recv()


N_COPIES = 140


def step_kernel(
    lookups_ref, counts_ref, slab_ref, ids_ref, label_ref, sw_ref, bias_ref, wout_ref,
    w_any, accum_any,
    ga_out, aa_out, arrived_ref, rids_ref, scale_ref, grad_ref,
    W, A, idsend, G, fac, hidden, dact, pacc, lg, LR, DL, gb, go, sv, rv,
    ZS, Df, ZRL, ZRR, ZL, ZR, DPL,
    R0, SB, RL, RV, Q, RL2, RV2,
    GA, AA, acc, slots, ns, NR,
    ssem, rsem, bulk, local,
):
    x, y, c, z = position()
    dp = (x * 4 + y) * 2 + c
    me = dp * 4 + z
    cp = Copies(ssem, rsem)
    go_to = cp.go
    zr, zl, zo = (z + 1) % 4, (z + 3) % 4, (z + 2) % 4
    xr, xl, xo = (x + 1) % 4, (x + 3) % 4, (x + 2) % 4
    yr, yl, yo = (y + 1) % 4, (y + 3) % 4, (y + 2) % 4
    LO, HI = slice(0, 1024), slice(1024, 2048)

    barrier = pltpu.get_barrier_semaphore()

    def greet(i, carry):
        pl.semaphore_signal(
            barrier, inc=1, device_id=place((me + i) % 128), device_id_type=MESH
        )
        return carry

    lax.fori_loop(1, 128, greet, 0)
    fetch_a = pltpu.make_async_copy(accum_any, A, local.at[1])
    fetch_a.start()
    fetch_w = pltpu.make_async_copy(w_any, W, local.at[0])
    fetch_w.start()

    starts, ends = owner_bounds(counts_ref)
    own_rows = pl.ds(pl.multiple_of(z * 256, 256), 256)

    def gather_pair(k):
        lane = iota((256, 128), 1)
        got = []
        for side in range(2):
            slot = slot_rows(lookups_ref[2 * k + side : 2 * k + side + 1, :], starts, ends)
            column = as_column(slot)
            half = jnp.floor(column * 0.5)
            odd = column - 2.0 * half
            both = mm(tiles_over_lanes(half, 16), slab_ref[...], 1, 0)
            one = jnp.where((lane >= 64) == (odd > 0.5), both, 0.0)
            got.append(one + pltpu.roll(one, 64, 1))
        G[own_rows, k * 128 : k * 128 + 128] = jnp.where(lane < 64, got[0], got[1]).astype(BF16)

    def block(src, k):
        return G.at[pl.ds(pl.multiple_of(src * 256, 256), 256), k * 256 : k * 256 + 256]

    def send_ids(i, carry):
        p = (me + i) % 128
        pltpu.make_async_remote_copy(
            src_ref=idsend.at[p], dst_ref=rids_ref.at[me], send_sem=bulk.at[0],
            recv_sem=bulk.at[1], device_id=place(p), device_id_type=MESH,
        ).start()
        return carry

    right, left = {}, {}

    def send_block(k):
        right[k] = go_to(block(z, k), block(z, k), {"mp": zr})
        left[k] = go_to(block(z, k), block(z, k), {"mp": zl})

    gather_pair(0)
    gather_pair(1)
    turned = jnp.concatenate([ids_ref[...].astype(F32), jnp.zeros((96, 128), F32)], axis=0)
    idsend[...] = turned.T.astype(I32).reshape(128, 1, 128)
    fetch_a.wait()
    AA[x, y, c] = A[...].astype(BF16)
    pl.semaphore_wait(barrier, 127)
    send_block(0)
    aa = Spread(AA, go_to, (x, y, c, z))
    aa.first()
    lax.fori_loop(1, 128, send_ids, 0)
    rids_ref[me] = idsend[me]
    gather_pair(4)
    gather_pair(5)
    send_block(2)
    gather_pair(2)
    gather_pair(3)
    send_block(1)
    gather_pair(6)
    gather_pair(7)
    send_block(3)
    fetch_w.wait()

    def forward(src):
        rows = pl.ds(pl.multiple_of(src * 256, 256), 256)
        pacc[...] = jnp.zeros_like(pacc)

        def tile(t, carry):
            cols = pl.ds(pl.multiple_of(t * 512, 512), 512)
            a = mm(G[rows, :], W[:, cols], 1, 0) + bias_ref[:, cols]
            wo = wout_ref[:, cols]
            sg = lax.logistic(a)
            h = (a * sg).astype(BF16)
            hidden[rows, cols] = h
            fac[src, :, :, :, cols] = (wo * sg * (1.0 + a * (1.0 - sg))).reshape(4, 2, 32, 512)
            m = h.astype(F32) * wo
            pacc[...] += (m[:, 0:128] + m[:, 128:256]) + (m[:, 256:384] + m[:, 384:512])
            return carry

        lax.fori_loop(0, 4, tile, 0)
        for s in range(2):
            line = jnp.sum(pacc[128 * s : 128 * s + 128, :].T, axis=0, keepdims=True)
            lg[pl.ds(src * 2 + s, 1), :] = line

    right[0].wait_recv()
    f0 = go_to(block(zl, 0), block(zl, 0), {"mp": zr})
    left[2].wait_recv()
    f2 = go_to(block(zr, 2), block(zr, 2), {"mp": zl})
    forward(z)
    right[1].wait_recv()
    f1 = go_to(block(zl, 1), block(zl, 1), {"mp": zr})
    left[3].wait_recv()
    f3 = go_to(block(zr, 3), block(zr, 3), {"mp": zl})
    aa.second()
    right[2].wait_recv()
    right[3].wait_recv()
    forward(zl)
    aa.third()
    left[0].wait_recv()
    left[1].wait_recv()
    forward(zr)
    aa.fourth()
    for copy in (f0, f1, f2, f3):
        copy.wait_recv()
    forward(zo)

    sent = [go_to(lg, LR.at[z], {"mp": (z + d) % 4}) for d in (1, 2, 3)]
    LR[z] = lg[...]
    for copy in sent:
        copy.wait_recv()
    logit = (LR[0] + LR[1]) + (LR[2] + LR[3])
    DL[...] = sw_ref[...] * (lax.logistic(logit) - label_ref[...].astype(F32))

    gb[...] = jnp.zeros_like(gb)
    go[...] = jnp.zeros_like(go)

    def dact_part(g, carry):
        rows = pl.ds(pl.multiple_of(g * 128, 128), 128)
        col = jnp.broadcast_to(DL[pl.ds(g, 1), :], (128, 128)).T
        for t in range(16):
            cols = slice(128 * t, 128 * t + 128)
            f = fac[g // 2, pl.ds((g % 2) * 2, 2), :, :, cols].reshape(128, 128)
            d = (f * col).astype(BF16)
            dact[rows, cols] = d
            gb[:, cols] += jnp.sum(d.astype(F32).reshape(16, 8, 128), axis=0)
            m = hidden[rows, cols].astype(F32) * col
            go[:, cols] += jnp.sum(m.reshape(16, 8, 128), axis=0)
        return carry

    lax.fori_loop(0, 8, dact_part, 0)

    def dpool(dest, put):
        rows = pl.ds(pl.multiple_of(dest * 256, 256), 256)

        def tile(t, carry):
            at = pl.multiple_of(t * 512, 512)
            put(mm(dact[rows, :], W[pl.ds(at, 512), :], 1, 1), pl.ds(at, 512))
            return carry

        lax.fori_loop(0, 2, tile, 0)

    def put_far(d, cols):
        ZS[0, :, cols] = d.astype(BF16)

    dpool(zo, put_far)
    z1 = go_to(ZS.at[0, 0:128], ZRL, {"mp": zr})
    z2 = go_to(ZS.at[0, 128:256], ZRR, {"mp": zl})

    def put_right(d, cols):
        Df[0, :, cols] = d[0:128]
        ZS[1, 128:256, cols] = d[128:256].astype(BF16)

    dpool(zr, put_right)
    z3 = go_to(ZS.at[1, 128:256], ZL.at[128:256], {"mp": zr})

    def put_left(d, cols):
        ZS[2, 0:128, cols] = d[0:128].astype(BF16)
        Df[1, :, cols] = d[128:256]

    dpool(zl, put_left)
    z4 = go_to(ZS.at[2, 0:128], ZR.at[0:128], {"mp": zl})

    partner = {"dp_2": 1 - c}
    to_core = {}

    def weight_grad(xi, tag):
        at = pl.multiple_of(xi * 256, 256)

        def tile(t, carry):
            cols = pl.ds(pl.multiple_of(t * 512, 512), 512)
            g = mm(G[:, pl.ds(at, 256)], dact[:, cols], 0, 0)
            fac[xi, :, :, :, cols] = g.reshape(4, 2, 32, 512)
            return carry

        lax.fori_loop(0, 4, tile, 0)
        to_core[tag] = go_to(fac.at[xi, :, 1 - c], R0.at[xi], partner)

    def chip_sum(xi, tag):
        to_core[tag].wait_recv()
        for yi in range(4):
            s = R0[xi, yi] + fac[xi, yi, c]
            R0[xi, yi] = s
            SB[xi, yi] = s.astype(BF16)

    weight_grad(xo, "o")
    weight_grad(xr, "r")
    chip_sum(xo, "o")
    h0a = go_to(SB.at[xo, 0:2, :, LO], RL.at[0, 0], {"dp_0": xr})
    h0b = go_to(SB.at[xo, 2:4, :, LO], RL.at[0, 1], {"dp_0": xl})
    z1.wait_recv()
    ZS[1, 0:128, :] = (Df[0] + ZRL[...].astype(F32)).astype(BF16)
    z5 = go_to(ZS.at[1, 0:128], ZL.at[0:128], {"mp": zr})
    z2.wait_recv()
    ZS[2, 128:256, :] = (Df[1] + ZRR[...].astype(F32)).astype(BF16)
    z6 = go_to(ZS.at[2, 128:256], ZR.at[128:256], {"mp": zl})
    weight_grad(xl, "l")
    chip_sum(xr, "r")
    h0c = go_to(SB.at[xr, 2:4, :, LO], RV.at[0, 0, 2:4], {"dp_0": xr})
    weight_grad(x, "m")
    chip_sum(xl, "l")
    h0d = go_to(SB.at[xl, 0:2, :, LO], RV.at[0, 1, 0:2], {"dp_0": xl})
    chip_sum(x, "m")
    h1a = go_to(SB.at[0:2, yo, :, HI], RL.at[1, 0], {"dp_1": yr})
    h1b = go_to(SB.at[2:4, yo, :, HI], RL.at[1, 1], {"dp_1": yl})
    h1c = go_to(SB.at[2:4, yr, :, HI], RV.at[1, 0, 2:4], {"dp_1": yr})
    h1d = go_to(SB.at[0:2, yl, :, HI], RV.at[1, 1, 0:2], {"dp_1": yl})

    h0a.wait_recv()
    for k in range(2):
        SB[xr, k, :, LO] = (R0[xr, k, :, LO] + RL[0, 0, k].astype(F32)).astype(BF16)
    h0e = go_to(SB.at[xr, 0:2, :, LO], RV.at[0, 0, 0:2], {"dp_0": xr})
    h0b.wait_recv()
    for k in range(2):
        SB[xl, 2 + k, :, LO] = (R0[xl, 2 + k, :, LO] + RL[0, 1, k].astype(F32)).astype(BF16)
    h0f = go_to(SB.at[xl, 2:4, :, LO], RV.at[0, 1, 2:4], {"dp_0": xl})

    for t in range(16):
        cols = slice(128 * t, 128 * t + 128)
        sv[t] = jnp.sum(gb[:, cols], axis=0, keepdims=True)
        sv[16 + t] = jnp.sum(go[:, cols], axis=0, keepdims=True)

    def send_small(i, carry):
        p = (dp + i) % 32
        where = {"dp_0": p // 8, "dp_1": (p // 2) % 4, "dp_2": p % 2, "mp": z}
        pltpu.make_async_remote_copy(
            src_ref=sv.at[p], dst_ref=rv.at[dp], send_sem=bulk.at[2],
            recv_sem=bulk.at[3], device_id=where, device_id_type=MESH,
        ).start()
        return carry

    lax.fori_loop(1, 32, send_small, 0)
    rv[dp] = sv[dp]

    def put_own(d, cols):
        DPL[:, cols] = d

    dpool(z, put_own)
    h1a.wait_recv()
    for k in range(2):
        SB[k, yr, :, HI] = (R0[k, yr, :, HI] + RL[1, 0, k].astype(F32)).astype(BF16)
    h1e = go_to(SB.at[0:2, yr, :, HI], RV.at[1, 0, 0:2], {"dp_1": yr})
    h1b.wait_recv()
    for k in range(2):
        SB[2 + k, yl, :, HI] = (R0[2 + k, yl, :, HI] + RL[1, 1, k].astype(F32)).astype(BF16)
    h1f = go_to(SB.at[2:4, yl, :, HI], RV.at[1, 1, 2:4], {"dp_1": yl})
    aa.fifth()

    def ring(h, axis, n):
        nr, nl, no = (n + 1) % 4, (n + 3) % 4, (n + 2) % 4
        s1 = go_to(Q.at[h, no, 0:16], RL2.at[h, 0], {axis: nr})
        s2 = go_to(Q.at[h, no, 16:32], RL2.at[h, 1], {axis: nl})
        s3 = go_to(Q.at[h, nr, 16:32], RV2.at[h, 0, 16:32], {axis: nr})
        s4 = go_to(Q.at[h, nl, 0:16], RV2.at[h, 1, 0:16], {axis: nl})
        return nr, nl, (s1, s2, s3, s4)

    def ring_relay(h, axis, state):
        nr, nl, (s1, s2, s3, s4) = state
        s1.wait_recv()
        Q[h, nr, 0:16] = Q[h, nr, 0:16] + RL2[h, 0]
        s5 = go_to(Q.at[h, nr, 0:16], RV2.at[h, 0, 0:16], {axis: nr})
        s2.wait_recv()
        Q[h, nl, 16:32] = Q[h, nl, 16:32] + RL2[h, 1]
        s6 = go_to(Q.at[h, nl, 16:32], RV2.at[h, 1, 16:32], {axis: nl})
        return s3, s4, s5, s6

    def segment(first, last):
        def pair(k, carry):
            lane = iota((256, 128), 1)
            block = DPL[:, pl.ds(pl.multiple_of(k * 128, 128), 128)]
            turned = pltpu.roll(block, 64, 1)
            hots, rows = [], []
            for side in range(2):
                slot = slot_rows(lookups_ref[pl.ds(2 * k + side, 1), :], starts, ends)
                low = slot - 16.0 * jnp.floor(slot * (1.0 / 16.0))
                upper = jnp.floor(slot * (1.0 / 16.0)) - 2.0 * jnp.floor(slot * (1.0 / 32.0))
                hots.append(
                    tiles_over_rows(16.0 * jnp.floor(slot * (1.0 / 32.0)) + low, 128)
                )
                upper = as_column(upper)
                same = jnp.where((lane < 64) == (side == 0), block, turned)
                kept = jnp.where((lane >= 64) == (upper > 0.5), same, 0.0)
                high = kept.astype(BF16)
                rest = (kept - high.astype(F32)).astype(BF16)
                rows.append(jnp.concatenate([high, rest], axis=1))
            part = mm(jnp.concatenate(hots, axis=1), jnp.concatenate(rows, axis=0), 1, 0)
            acc[...] += part
            return carry

        lax.fori_loop(first, last, pair, 0)

    for copy in (z3, z4, z5, z6):
        copy.wait_recv()
    DPL[...] = DPL[...] + (ZL[...].astype(F32) + ZR[...].astype(F32))
    acc[...] = jnp.zeros_like(acc)
    segment(0, 1)
    for copy in (h0c, h0d, h0e, h0f):
        copy.wait_recv()
    for k in range(4):
        Q[0, k] = R0[x, k, :, LO] + (RV[0, 0, k].astype(F32) + RV[0, 1, k].astype(F32))
    t0 = ring(0, "dp_1", y)
    segment(1, 3)
    for copy in (h1c, h1d, h1e, h1f):
        copy.wait_recv()
    for k in range(4):
        Q[1, k] = R0[k, y, :, HI] + (RV[1, 0, k].astype(F32) + RV[1, 1, k].astype(F32))
    t1 = ring(1, "dp_0", x)
    u0 = ring_relay(0, "dp_1", t0)
    segment(3, 5)
    u1 = ring_relay(1, "dp_0", t1)
    segment(5, 8)
    total = acc[:, :128] + acc[:, 128:]
    slots[...] = total.astype(BF16).reshape(128, 16, 128)
    few = jnp.sum((total * total).reshape(256, 8, 128), axis=0)

    def send_slots(i, carry):
        p = (me + i) % 128
        pltpu.make_async_remote_copy(
            src_ref=slots.at[p], dst_ref=arrived_ref.at[me], send_sem=bulk.at[4],
            recv_sem=bulk.at[5], device_id=place(p), device_id_type=MESH,
        ).start()
        return carry

    for copy in u0 + u1:
        copy.wait_recv()
    lower = Q[0, y] + (RV2[0, 0] + RV2[0, 1])
    upper = Q[1, x] + (RV2[1, 0] + RV2[1, 1])
    grad_ref[:, LO] = lower
    grad_ref[:, HI] = upper
    GA[x, y, c, :, LO] = lower.astype(BF16)
    GA[x, y, c, :, HI] = upper.astype(BF16)
    ga = Spread(GA, go_to, (x, y, c, z))
    ga.first()
    both = lower * lower + upper * upper
    both = jnp.sum(both.reshape(4, 8, 1024), axis=0)
    for t in range(8):
        few = few + both[:, 128 * t : 128 * t + 128]
    small = sv.at[pl.ds(0, 31)]
    pltpu.make_async_copy(small, small, bulk.at[2]).wait()
    pltpu.make_async_copy(small, small, bulk.at[3]).wait()
    bias_sum = jnp.sum(rv[...], axis=0)
    ns[...] = jnp.sum(few, axis=0, keepdims=True) + bias_sum * bias_sum

    def send_norm(i, carry):
        p = (me + i) % 128
        pltpu.make_async_remote_copy(
            src_ref=ns, dst_ref=NR.at[me], send_sem=bulk.at[6],
            recv_sem=bulk.at[7], device_id=place(p), device_id_type=MESH,
        ).start()
        return carry

    lax.fori_loop(1, 128, send_norm, 0)
    lax.fori_loop(1, 128, send_slots, 0)
    NR[me] = ns[...]
    arrived_ref[me] = slots[me]
    aa.last()
    put_aa = pltpu.make_async_copy(AA, aa_out, local.at[2])
    put_aa.start()
    ga.second()
    ga.third()
    ga.fourth()
    lot = NR.at[pl.ds(0, 127)]
    pltpu.make_async_copy(lot, lot, bulk.at[7]).wait()
    lanes = jnp.sum(NR[...], axis=0)
    norm = jnp.sum(lanes, axis=1, keepdims=True)
    scale = clip_norm / jnp.maximum(jnp.sqrt(norm), clip_norm)
    scale_ref[...] = jnp.broadcast_to(scale, (8, 128))
    ga.fifth()
    many = arrived_ref.at[pl.ds(0, 127)]
    pltpu.make_async_copy(many, many, bulk.at[5]).wait()
    ga.last()
    put_ga = pltpu.make_async_copy(GA, ga_out, local.at[3])
    put_ga.start()
    pltpu.make_async_copy(lot, lot, bulk.at[6]).wait()
    pltpu.make_async_copy(many, many, bulk.at[4]).wait()
    lot = idsend.at[pl.ds(0, 127)]
    pltpu.make_async_copy(lot, lot, bulk.at[0]).wait()
    pltpu.make_async_copy(lot, lot, bulk.at[1]).wait()
    cp.drain()
    put_aa.wait()
    put_ga.wait()


def finish_kernel(
    arrived_ref, rids_ref, scale_ref, table_ref, accum_ref, grad_ref, dense_ref,
    ga_any, aa_any, w_any,
    new_ref, accum_new_ref, dense_new_ref, wn_any,
    acc, ids, GA, AA, W, WN, sem, osem,
):
    chunk = 128
    count = 1024 // chunk
    loads = []
    for i in range(count):
        rows = pl.ds(i * chunk, chunk)
        for j, (src, dst) in enumerate(((ga_any, GA), (aa_any, AA), (w_any, W))):
            copy = pltpu.make_async_copy(src.at[rows], dst.at[rows], sem.at[i, j])
            copy.start()
            loads.append(copy)
    scale = scale_ref[0:1, 0:1]
    clipped = scale * grad_ref[...]
    dense_new_ref[...] = dense_ref[...] + clipped * clipped

    lane16 = iota((16, 128), 1) // 16
    for upper in range(2):
        lined = jnp.zeros((16, 128), F32)
        for d in range(8):
            piece = rids_ref[:, d, :].astype(F32)
            lined = jnp.where(lane16 == d, pltpu.roll(piece, (16 * d - 16 * upper) % 128, 1), lined)
        ids[upper] = lined

    pairs = acc.shape[0]
    acc[...] = jnp.zeros_like(acc)
    step = 256

    def part(t, carry):
        lane = iota((step, 128), 1)
        base = pl.multiple_of(t * step, step)
        block = arrived_ref[pl.ds(base, step), :].astype(F32)
        turned = pltpu.roll(block, 64, 1)
        hots, values = [], []
        for side in range(2):
            row = jnp.concatenate(
                [ids[side, pl.ds(2 * t, 1), :], ids[side, pl.ds(2 * t + 1, 1), :]], axis=1
            )
            above = row >= float(pairs)
            hots.append(tiles_over_rows(jnp.where(above, row - float(pairs), row), pairs // 16))
            high = as_column(jnp.where(above, 1.0, 0.0))
            same = jnp.where((lane < 64) == (side == 0), block, turned)
            values.append(jnp.where((lane >= 64) == (high > 0.5), same, 0.0).astype(BF16))
        acc[...] += mm(jnp.concatenate(hots, axis=1), jnp.concatenate(values, axis=0), 1, 0)
        return carry

    lax.fori_loop(0, arrived_ref.shape[0] // step, part, 0)
    for p in range(pairs // 128):
        both = acc[128 * p : 128 * p + 128, :].T * scale
        for upper in range(2):
            r = both[64 * upper : 64 * upper + 64, :]
            line = p + upper * (pairs // 128)
            fresh = accum_ref[line : line + 1, :] + jnp.sum(r * r, axis=0, keepdims=True) / 64.0
            accum_new_ref[line : line + 1, :] = fresh
            at = line * 128
            new_ref[:, at : at + 128] = table_ref[:, at : at + 128] - table_rate * r / (
                jnp.sqrt(fresh) + adagrad_eps
            )

    for copy in loads:
        copy.wait()

    def weights(i, carry):
        rows = pl.ds(pl.multiple_of(i * chunk, chunk), chunk)

        def tile(t, carry):
            cols = pl.ds(pl.multiple_of(t * 512, 512), 512)
            g = scale * GA[rows, cols].astype(F32)
            fresh = AA[rows, cols].astype(F32) + g * g
            WN[rows, cols] = (
                W[rows, cols].astype(F32) - dense_rate * g / (jnp.sqrt(fresh) + adagrad_eps)
            ).astype(BF16)
            return carry

        lax.fori_loop(0, 4, tile, 0)
        pltpu.make_async_copy(WN.at[rows], wn_any.at[rows], osem).start()
        return carry

    lax.fori_loop(0, count, weights, 0)
    pltpu.make_async_copy(WN, wn_any, osem).wait()


def shape(dims, kind):
    return jax.ShapeDtypeStruct(dims, kind)


def body(
    slab_values,
    row_ids,
    peer_counts,
    lookup_slots,
    labels,
    sample_weight,
    weight_in,
    bias_in,
    weight_out,
    dense_accum,
    table_rows,
    table_accum,
):
    V = pltpu.VMEM
    DMA = pltpu.SemaphoreType.DMA
    whole = (4, 4, 2, 32, 2048)
    ga, aa, arrived, rids, scale, grad = pl.pallas_call(
        step_kernel,
        out_shape=(
            shape(whole, BF16), shape(whole, BF16), shape((128, 16, 128), BF16),
            shape((128, 1, 128), I32), shape((8, 128), F32), shape((32, 2048), F32),
        ),
        in_specs=[VM] * 8 + [ANY] * 2,
        out_specs=(ANY, ANY, VM, VM, VM, VM),
        scratch_shapes=[
            V((1024, 2048), BF16), V((32, 2048), F32), V((128, 1, 128), I32),
            V((1024, 1024), BF16), V(whole, F32), V((1024, 2048), BF16),
            V((1024, 2048), BF16), V((256, 128), F32), V((8, 128), F32), V((4, 8, 128), F32),
            V((8, 128), F32), V((8, 2048), F32), V((8, 2048), F32),
            V((32, 1, 128), F32), V((32, 1, 128), F32),
            V((3, 256, 1024), BF16), V((2, 128, 1024), F32),
            V((128, 1024), BF16), V((128, 1024), BF16),
            V((256, 1024), BF16), V((256, 1024), BF16), V((256, 1024), F32),
            V((4, 4, 32, 2048), F32), V((4, 4, 32, 2048), BF16),
            V((2, 2, 2, 32, 1024), BF16), V((2, 2, 4, 32, 1024), BF16),
            V((2, 4, 32, 1024), F32), V((2, 2, 16, 1024), F32), V((2, 2, 32, 1024), F32),
            V(whole, BF16), V(whole, BF16), V((2048, 256), F32), V((128, 16, 128), BF16),
            V((1, 128), F32), V((128, 1, 128), F32),
            DMA((N_COPIES,)), DMA((N_COPIES,)), DMA((8,)), DMA((4,)),
        ],
        compiler_params=pltpu.CompilerParams(
            has_side_effects=True, vmem_limit_bytes=63 * 1024 * 1024, collective_id=0
        ),
        name="step",
    )(
        lookup_slots.T,
        peer_counts,
        slab_values[0].reshape(2048, 128),
        row_ids[0].T,
        labels.reshape(8, 128),
        sample_weight.reshape(8, 128),
        bias_in.reshape(1, 2048),
        weight_out.astype(F32).reshape(1, 2048),
        weight_in,
        dense_accum,
    )
    table_new, table_accum_new, accum_new, weight_new = pl.pallas_call(
        finish_kernel,
        out_shape=(
            shape((64, 4096), F32), shape((32, 128), F32), shape((32, 2048), F32),
            shape((1024, 2048), BF16),
        ),
        in_specs=[VM] * 7 + [ANY] * 3,
        out_specs=(VM, VM, VM, ANY),
        scratch_shapes=[
            V((2048, 128), F32), V((2, 16, 128), F32),
            V((1024, 2048), BF16), V((1024, 2048), BF16), V((1024, 2048), BF16),
            V((1024, 2048), BF16), DMA((8, 3)), DMA,
        ],
        name="finish",
    )(
        arrived.reshape(2048, 128),
        rids.reshape(16, 8, 128),
        scale,
        table_rows.T,
        table_accum.reshape(32, 128),
        grad,
        dense_accum,
        ga.reshape(1024, 2048),
        aa.reshape(1024, 2048),
        weight_in,
    )
    return (weight_new, accum_new, table_new.T, table_accum_new.reshape(4096))


def solution(mesh):
    torus = Mesh(mesh.devices.reshape(4, 4, 2, mesh.shape["mp"]), ("dp_0", "dp_1", "dp_2", "mp"))
    placed = (
        P(DP_MP, None, None),
        P(DP_MP, None, None),
        P(DP_MP, None),
        P(DP_MP, None),
        P(DP),
        P(DP),
        P(None, "mp"),
        P("mp"),
        P("mp"),
        P(DP, "mp"),
        P(DP_MP, None),
        P(DP_MP),
    )
    return jax.shard_map(
        body,
        mesh=torus,
        in_specs=placed,
        out_specs=(P(None, "mp"), P(DP, "mp"), P(DP_MP, None), P(DP_MP)),
        check_vma=False,
    )
```

time: 329 us -> 141 us (0.43)
  Pallas kernels: 0 us -> 136 us
  waiting for transfers between devices: 96.5 us -> 0 us
  other arithmetic: 77.7 us -> 1.29 us
  local copies, waits for them, and re-layouts: 42.7 us -> 2.07 us
  blocking collectives: 31.6 us -> 0 us
  matrix products: 30.9 us -> 0 us
  starting transfers between devices: 30.5 us -> 0 us
  between operations: 17.7 us -> 0.8 us
    pallas_call x0 -> x2, Pallas kernels: none -> 136 us  [the longest x1 120 us: body(): pl.pallas_call(step_kernel, out_shape=(shape(whole, BF16), shape(whole, B...]
    all_to_all x5 -> x0, waiting for transfers between devices: 96.4 us -> none  [the longest x1 46.6 us: sum_at_owner(): lax.all_to_all(pieces, axis, split_axis=0, concat_axis=0, tiled=True)]
    scatter-add x2 -> x0, other arithmetic: 46.4 us -> none  [the longest x1 23.2 us: body(): jax.ops.segment_sum(arrived.reshape(-1, emb_width), arrived_rows.reshape(...]
    psum x4 -> x0, blocking collectives: 31.6 us -> none  [over_axes(): return functools.reduce(lax.psum, axes, shard)]
    dot_general x5 -> x0, matrix products: 30.9 us -> none  [the longest x1 10.4 us: body(): lax.dot_general(dact, weight_in, (((1,), (1,)), ((), ())), preferred_elem...]
    all_to_all x5 -> x0, starting transfers between devices: 30.1 us -> none  [the longest x3 19.3 us: from_everyone(): lax.all_to_all(jnp.broadcast_to(shard[None], (length, *shard.shape)), axi...]
    reduce_sum x10 -> x0, other arithmetic: 24.7 us -> none  [the longest x1 5.96 us: body(): grad_bias = jnp.sum(dact.astype(jnp.float32), axis=0)]
    unnamed x30 -> x0, local copies, waits for them, and re-layouts: 14 us -> none
  transfers between devices with their start and end apart: 7 -> 0, of which waited for: 5 -> 0; matrix products, arithmetic and copies ran while one was open for 26% -> 0% of each run, Pallas kernels for 0% -> 0%
where the time goes in v2:
time: 141 us; the launch traced here: 140 us
  Pallas kernels  136 us (96%)
  local copies, waits for them, and re-layouts  2.07 us (1%)
    pallas_call x1, Pallas kernels, body(): pl.pallas_call(step_kernel, out_shape=(shape(whole, BF16), shape(whole, B...  120 us
    pallas_call x1, Pallas kernels, body(): pl.pallas_call(finish_kernel, out_shape=(shape((64, 4096), F32), shape((3...  16.6 us

profile of v2, /device:TPU:1, one launch (start us, length us, event | category | flops | bytes accessed | tf_op | source)
XLA Modules:
  0.0 140.3 jit_solution(8908946869844264849)
XLA Ops:
  0.6 1.3 reshape.51
  1.9 2.1 %reshape_squeeze.3.slab_ref = bf16[2048,128]{1,0:T(8,128)(2,1)} reshape(bf16[1,128,2048]{2,1,0:T(8,128)(2,1)} %param.12) | data formatting | bytes 1048576 | tf_op jit(solution)/shard_map/reshape;squeeze | solution.py:749
  4.0 119.5 %step.1 = (bf16[4,4,2,32,2048]{4,3,2,1,0:T(8,128)(2,1)}, bf16[4,4,2,32,2048]{4,3,2,1,0:T(8,128)(2,1)}, bf16[128,16,128]{2,1,0:T(8,128)(2,1)}, s32[128,1,128]{2,1...) custom-call(s32[16,256]{1,0:T(8,128)} %bitcast.22, s32[1,128]{1,0:T(1,128)} %counts_ref.1, ...), custom_call_target="tpu_custom_call" | custom-call | tf_op jit(solution)/shard_map/step/pallas_call | solution.py:718
  123.5 16.6 %finish.1 = (f32[64,4096]{1,0:T(8,128)}, f32[32,128]{1,0:T(8,128)}, f32[32,2048]{1,0:T(8,128)}, bf16[1024,2048]{1,0:T(8,128)(2,1)}) custom-call(bf16[2048,128]{1,0:T(8,128)(2,1)} %bitcast.19, s32[16,8,128]{2,1,0:T(8,128)} %bitcast.20, f32[8,128]{1,0:T(8,128)} %get-tuple-element.16.scale_ref, f32[64,4096]{1,0:T(8,128)} %bitcast.18, f32[32,128]{1,0:T(8,128)} %bitcast.24, ...), custom_call_target="tpu_custom_call" | custom-call | tf_op jit(solution)/shard_map/finish/pallas_call | solution.py:758

commit v3 on v2

--- a/solution.py
+++ b/solution.py
@@ -20,6 +20,7 @@
 BF16 = jnp.bfloat16
 I32 = jnp.int32
 MESH = pl.DeviceIdType.MESH
+LOGICAL = pl.DeviceIdType.LOGICAL
 VM = pl.BlockSpec(memory_space=pltpu.VMEM)
 ANY = pl.BlockSpec(memory_space=pl.ANY)
 
@@ -36,13 +37,17 @@
     return tuple(lax.axis_index(a) for a in DP_MP)
 
 
-def place(index):
-    return {
-        "dp_0": index // 32,
-        "dp_1": (index // 8) % 4,
-        "dp_2": (index // 4) % 2,
-        "mp": index % 4,
-    }
+def to_all(me, emit):
+    for u in range(1, 8):
+        emit(lax.rem(me + u, 128))
+
+    def more(j, carry):
+        base = me + 8 * j
+        for u in range(8):
+            emit(lax.rem(base + u, 128))
+        return carry
+
+    lax.fori_loop(1, 16, more, 0)
 
 
 class Copies:
@@ -123,13 +128,31 @@
     LO, HI = slice(0, 1024), slice(1024, 2048)
     T, B = slice(0, 16), slice(16, 32)
 
-    def __init__(self, ref, go, where):
-        self.ref, self.go = ref, go
+    def __init__(self, ref, go, where, out, sem):
+        self.ref, self.go, self.out, self.sem, self.written = ref, go, out, sem, []
         self.x, self.y, self.c, _ = where
         self.xr, self.xl, self.xo = ((self.x + d) % 4 for d in (1, 3, 2))
         self.yr, self.yl, self.yo = ((self.y + d) % 4 for d in (1, 3, 2))
         self.partner = {"dp_2": 1 - self.c}
-        self.d = []
+        self.d, self.pieces = [], []
+
+    def across(self, *pieces):
+        for piece in pieces:
+            self.d.append(self.same(piece, self.partner))
+            self.pieces.append(piece)
+            self.write(piece)
+
+    def from_partner(self, first, last):
+        for k in range(first, last):
+            self.d[k].wait_recv()
+            a, b, _, rows, cols = self.pieces[k]
+            self.write((a, b, 1 - self.c, rows, cols))
+
+    def write(self, piece):
+        k = len(self.written)
+        copy = pltpu.make_async_copy(self.ref.at[piece], self.out.at[piece], self.sem.at[k])
+        copy.start()
+        self.written.append(copy)
 
     def same(self, piece, where):
         ref = self.ref.at[piece]
@@ -166,7 +189,7 @@
         self.q4.wait_recv()
         self.q5 = self.same(other, {"dp_0": self.xr})
         self.q6 = self.same(other, {"dp_0": self.xl})
-        self.d += [self.same(mine, self.partner), self.same(other, self.partner)]
+        self.across(mine, other)
 
     def fourth(self):
         c = self.c
@@ -179,22 +202,27 @@
         self.q7 = self.same((self.xl, slice(0, 2), c, every, self.HI), {"dp_0": self.xr})
         self.q6.wait_recv()
         self.q8 = self.same((self.xr, slice(2, 4), c, every, self.HI), {"dp_0": self.xl})
-        for n in (self.yl, self.yr):
-            self.d.append(self.same((every, n, c, every, self.LO), self.partner))
-        for n in (self.xl, self.xr):
-            self.d.append(self.same((n, every, c, every, self.HI), self.partner))
+        self.across(*((every, n, c, every, self.LO) for n in (self.yl, self.yr)))
+        self.across(*((n, every, c, every, self.HI) for n in (self.xl, self.xr)))
+        self.from_partner(0, 2)
 
     def fifth(self):
         c = self.c
         every = slice(None)
-        for copy in (self.p7, self.p8, self.q7, self.q8):
-            copy.wait_recv()
-        self.d.append(self.same((every, self.yo, c, every, self.LO), self.partner))
-        self.d.append(self.same((self.xo, every, c, every, self.HI), self.partner))
+        self.p7.wait_recv()
+        self.p8.wait_recv()
+        self.across((every, self.yo, c, every, self.LO))
+        self.q7.wait_recv()
+        self.q8.wait_recv()
+        self.across((self.xo, every, c, every, self.HI))
+        self.from_partner(2, 6)
 
     def last(self):
-        for copy in self.d:
-            copy.wait_recv()
+        self.from_partner(6, 8)
+
+    def close(self):
+        for copy in self.written:
+            copy.wait()
 
 
 N_COPIES = 140
@@ -207,8 +235,8 @@
     W, A, idsend, G, fac, hidden, dact, pacc, lg, LR, DL, gb, go, sv, rv,
     ZS, Df, ZRL, ZRR, ZL, ZR, DPL,
     R0, SB, RL, RV, Q, RL2, RV2,
-    GA, AA, acc, slots, ns, NR,
-    ssem, rsem, bulk, local,
+    GA, AA, acc, slots, ns, NR, SC, slab, wout,
+    ssem, rsem, bulk, local, wsem,
 ):
     x, y, c, z = position()
     dp = (x * 4 + y) * 2 + c
@@ -222,13 +250,10 @@
 
     barrier = pltpu.get_barrier_semaphore()
 
-    def greet(i, carry):
-        pl.semaphore_signal(
-            barrier, inc=1, device_id=place((me + i) % 128), device_id_type=MESH
-        )
-        return carry
-
-    lax.fori_loop(1, 128, greet, 0)
+    def greet(p):
+        pl.semaphore_signal(barrier, inc=1, device_id=p, device_id_type=LOGICAL)
+
+    to_all(me, greet)
     fetch_a = pltpu.make_async_copy(accum_any, A, local.at[1])
     fetch_a.start()
     fetch_w = pltpu.make_async_copy(w_any, W, local.at[0])
@@ -245,7 +270,7 @@
             column = as_column(slot)
             half = jnp.floor(column * 0.5)
             odd = column - 2.0 * half
-            both = mm(tiles_over_lanes(half, 16), slab_ref[...], 1, 0)
+            both = mm(tiles_over_lanes(half, 16), slab[...], 1, 0)
             one = jnp.where((lane >= 64) == (odd > 0.5), both, 0.0)
             got.append(one + pltpu.roll(one, 64, 1))
         G[own_rows, k * 128 : k * 128 + 128] = jnp.where(lane < 64, got[0], got[1]).astype(BF16)
@@ -253,13 +278,11 @@
     def block(src, k):
         return G.at[pl.ds(pl.multiple_of(src * 256, 256), 256), k * 256 : k * 256 + 256]
 
-    def send_ids(i, carry):
-        p = (me + i) % 128
+    def send_ids(p):
         pltpu.make_async_remote_copy(
             src_ref=idsend.at[p], dst_ref=rids_ref.at[me], send_sem=bulk.at[0],
-            recv_sem=bulk.at[1], device_id=place(p), device_id_type=MESH,
+            recv_sem=bulk.at[1], device_id=p, device_id_type=LOGICAL,
         ).start()
-        return carry
 
     right, left = {}, {}
 
@@ -267,18 +290,19 @@
         right[k] = go_to(block(z, k), block(z, k), {"mp": zr})
         left[k] = go_to(block(z, k), block(z, k), {"mp": zl})
 
+    for k in range(16):
+        acc[pl.ds(k, 128, stride=16), :] = slab_ref[:, k * 128 : k * 128 + 128].astype(F32)
+    slab[...] = acc[...].astype(BF16)
+    for k in range(16):
+        wout[:, k * 128 : k * 128 + 128] = wout_ref[k : k + 1, :].astype(F32)
     gather_pair(0)
     gather_pair(1)
-    turned = jnp.concatenate([ids_ref[...].astype(F32), jnp.zeros((96, 128), F32)], axis=0)
-    idsend[...] = turned.T.astype(I32).reshape(128, 1, 128)
     fetch_a.wait()
     AA[x, y, c] = A[...].astype(BF16)
     pl.semaphore_wait(barrier, 127)
     send_block(0)
-    aa = Spread(AA, go_to, (x, y, c, z))
+    aa = Spread(AA, go_to, (x, y, c, z), aa_out, wsem.at[0])
     aa.first()
-    lax.fori_loop(1, 128, send_ids, 0)
-    rids_ref[me] = idsend[me]
     gather_pair(4)
     gather_pair(5)
     send_block(2)
@@ -288,6 +312,10 @@
     gather_pair(6)
     gather_pair(7)
     send_block(3)
+    turned = jnp.concatenate([ids_ref[...].astype(F32), jnp.zeros((96, 128), F32)], axis=0)
+    idsend[...] = turned.T.astype(I32).reshape(128, 1, 128)
+    to_all(me, send_ids)
+    rids_ref[me] = idsend[me]
     fetch_w.wait()
 
     def forward(src):
@@ -297,7 +325,7 @@
         def tile(t, carry):
             cols = pl.ds(pl.multiple_of(t * 512, 512), 512)
             a = mm(G[rows, :], W[:, cols], 1, 0) + bias_ref[:, cols]
-            wo = wout_ref[:, cols]
+            wo = wout[:, cols]
             sg = lax.logistic(a)
             h = (a * sg).astype(BF16)
             hidden[rows, cols] = h
@@ -324,11 +352,10 @@
     right[2].wait_recv()
     right[3].wait_recv()
     forward(zl)
-    aa.third()
     left[0].wait_recv()
     left[1].wait_recv()
     forward(zr)
-    aa.fourth()
+    aa.third()
     for copy in (f0, f1, f2, f3):
         copy.wait_recv()
     forward(zo)
@@ -340,23 +367,30 @@
     logit = (LR[0] + LR[1]) + (LR[2] + LR[3])
     DL[...] = sw_ref[...] * (lax.logistic(logit) - label_ref[...].astype(F32))
 
-    gb[...] = jnp.zeros_like(gb)
-    go[...] = jnp.zeros_like(go)
+    def column(g):
+        return jnp.broadcast_to(DL[pl.ds(g, 1), :], (128, 128)).T
 
     def dact_part(g, carry):
         rows = pl.ds(pl.multiple_of(g * 128, 128), 128)
-        col = jnp.broadcast_to(DL[pl.ds(g, 1), :], (128, 128)).T
+        col = column(g)
         for t in range(16):
             cols = slice(128 * t, 128 * t + 128)
             f = fac[g // 2, pl.ds((g % 2) * 2, 2), :, :, cols].reshape(128, 128)
-            d = (f * col).astype(BF16)
-            dact[rows, cols] = d
-            gb[:, cols] += jnp.sum(d.astype(F32).reshape(16, 8, 128), axis=0)
+            dact[rows, cols] = (f * col).astype(BF16)
+        return carry
+
+    lax.fori_loop(0, 8, dact_part, 0)
+
+    def sums_part(g, carry):
+        rows = pl.ds(pl.multiple_of(g * 128, 128), 128)
+        col = column(g)
+        for t in range(16):
+            cols = slice(128 * t, 128 * t + 128)
+            d = dact[rows, cols].astype(F32)
+            gb[:, cols] += jnp.sum(d.reshape(16, 8, 128), axis=0)
             m = hidden[rows, cols].astype(F32) * col
             go[:, cols] += jnp.sum(m.reshape(16, 8, 128), axis=0)
         return carry
-
-    lax.fori_loop(0, 8, dact_part, 0)
 
     def dpool(dest, put):
         rows = pl.ds(pl.multiple_of(dest * 256, 256), 256)
@@ -375,20 +409,6 @@
     z1 = go_to(ZS.at[0, 0:128], ZRL, {"mp": zr})
     z2 = go_to(ZS.at[0, 128:256], ZRR, {"mp": zl})
 
-    def put_right(d, cols):
-        Df[0, :, cols] = d[0:128]
-        ZS[1, 128:256, cols] = d[128:256].astype(BF16)
-
-    dpool(zr, put_right)
-    z3 = go_to(ZS.at[1, 128:256], ZL.at[128:256], {"mp": zr})
-
-    def put_left(d, cols):
-        ZS[2, 0:128, cols] = d[0:128].astype(BF16)
-        Df[1, :, cols] = d[128:256]
-
-    dpool(zl, put_left)
-    z4 = go_to(ZS.at[2, 0:128], ZR.at[0:128], {"mp": zl})
-
     partner = {"dp_2": 1 - c}
     to_core = {}
 
@@ -399,35 +419,49 @@
             cols = pl.ds(pl.multiple_of(t * 512, 512), 512)
             g = mm(G[:, pl.ds(at, 256)], dact[:, cols], 0, 0)
             fac[xi, :, :, :, cols] = g.reshape(4, 2, 32, 512)
+            SC[xi, :, :, cols] = fac[xi, :, 1 - c, :, cols].astype(BF16)
             return carry
 
         lax.fori_loop(0, 4, tile, 0)
-        to_core[tag] = go_to(fac.at[xi, :, 1 - c], R0.at[xi], partner)
+        to_core[tag] = go_to(SC.at[xi], R0.at[xi], partner)
 
     def chip_sum(xi, tag):
         to_core[tag].wait_recv()
         for yi in range(4):
-            s = R0[xi, yi] + fac[xi, yi, c]
-            R0[xi, yi] = s
+            s = R0[xi, yi].astype(F32) + fac[xi, yi, c]
+            fac[xi, yi, c] = s
             SB[xi, yi] = s.astype(BF16)
 
+    def put_right(d, cols):
+        Df[0, :, cols] = d[0:128]
+        ZS[1, 128:256, cols] = d[128:256].astype(BF16)
+
+    def put_left(d, cols):
+        ZS[2, 0:128, cols] = d[0:128].astype(BF16)
+        Df[1, :, cols] = d[128:256]
+
     weight_grad(xo, "o")
+    aa.fourth()
     weight_grad(xr, "r")
+    dpool(zr, put_right)
+    z3 = go_to(ZS.at[1, 128:256], ZL.at[128:256], {"mp": zr})
     chip_sum(xo, "o")
     h0a = go_to(SB.at[xo, 0:2, :, LO], RL.at[0, 0], {"dp_0": xr})
     h0b = go_to(SB.at[xo, 2:4, :, LO], RL.at[0, 1], {"dp_0": xl})
+    weight_grad(xl, "l")
+    dpool(zl, put_left)
+    z4 = go_to(ZS.at[2, 0:128], ZR.at[0:128], {"mp": zl})
+    chip_sum(xr, "r")
+    h0c = go_to(SB.at[xr, 2:4, :, LO], RV.at[0, 0, 2:4], {"dp_0": xr})
+    weight_grad(x, "m")
+    chip_sum(xl, "l")
+    h0d = go_to(SB.at[xl, 0:2, :, LO], RV.at[0, 1, 0:2], {"dp_0": xl})
     z1.wait_recv()
     ZS[1, 0:128, :] = (Df[0] + ZRL[...].astype(F32)).astype(BF16)
     z5 = go_to(ZS.at[1, 0:128], ZL.at[0:128], {"mp": zr})
     z2.wait_recv()
     ZS[2, 128:256, :] = (Df[1] + ZRR[...].astype(F32)).astype(BF16)
     z6 = go_to(ZS.at[2, 128:256], ZR.at[128:256], {"mp": zl})
-    weight_grad(xl, "l")
-    chip_sum(xr, "r")
-    h0c = go_to(SB.at[xr, 2:4, :, LO], RV.at[0, 0, 2:4], {"dp_0": xr})
-    weight_grad(x, "m")
-    chip_sum(xl, "l")
-    h0d = go_to(SB.at[xl, 0:2, :, LO], RV.at[0, 1, 0:2], {"dp_0": xl})
     chip_sum(x, "m")
     h1a = go_to(SB.at[0:2, yo, :, HI], RL.at[1, 0], {"dp_1": yr})
     h1b = go_to(SB.at[2:4, yo, :, HI], RL.at[1, 1], {"dp_1": yl})
@@ -436,13 +470,16 @@
 
     h0a.wait_recv()
     for k in range(2):
-        SB[xr, k, :, LO] = (R0[xr, k, :, LO] + RL[0, 0, k].astype(F32)).astype(BF16)
+        SB[xr, k, :, LO] = (fac[xr, k, c, :, LO] + RL[0, 0, k].astype(F32)).astype(BF16)
     h0e = go_to(SB.at[xr, 0:2, :, LO], RV.at[0, 0, 0:2], {"dp_0": xr})
     h0b.wait_recv()
     for k in range(2):
-        SB[xl, 2 + k, :, LO] = (R0[xl, 2 + k, :, LO] + RL[0, 1, k].astype(F32)).astype(BF16)
+        SB[xl, 2 + k, :, LO] = (fac[xl, 2 + k, c, :, LO] + RL[0, 1, k].astype(F32)).astype(BF16)
     h0f = go_to(SB.at[xl, 2:4, :, LO], RV.at[0, 1, 2:4], {"dp_0": xl})
 
+    gb[...] = jnp.zeros_like(gb)
+    go[...] = jnp.zeros_like(go)
+    lax.fori_loop(0, 8, sums_part, 0)
     for t in range(16):
         cols = slice(128 * t, 128 * t + 128)
         sv[t] = jnp.sum(gb[:, cols], axis=0, keepdims=True)
@@ -466,11 +503,11 @@
     dpool(z, put_own)
     h1a.wait_recv()
     for k in range(2):
-        SB[k, yr, :, HI] = (R0[k, yr, :, HI] + RL[1, 0, k].astype(F32)).astype(BF16)
+        SB[k, yr, :, HI] = (fac[k, yr, c, :, HI] + RL[1, 0, k].astype(F32)).astype(BF16)
     h1e = go_to(SB.at[0:2, yr, :, HI], RV.at[1, 0, 0:2], {"dp_1": yr})
     h1b.wait_recv()
     for k in range(2):
-        SB[2 + k, yl, :, HI] = (R0[2 + k, yl, :, HI] + RL[1, 1, k].astype(F32)).astype(BF16)
+        SB[2 + k, yl, :, HI] = (fac[2 + k, yl, c, :, HI] + RL[1, 1, k].astype(F32)).astype(BF16)
     h1f = go_to(SB.at[2:4, yl, :, HI], RV.at[1, 1, 2:4], {"dp_1": yl})
     aa.fifth()
 
@@ -512,7 +549,7 @@
                 rest = (kept - high.astype(F32)).astype(BF16)
                 rows.append(jnp.concatenate([high, rest], axis=1))
             part = mm(jnp.concatenate(hots, axis=1), jnp.concatenate(rows, axis=0), 1, 0)
-            acc[...] += part
+            acc[...] += part[:, :128] + part[:, 128:]
             return carry
 
         lax.fori_loop(first, last, pair, 0)
@@ -521,33 +558,31 @@
         copy.wait_recv()
     DPL[...] = DPL[...] + (ZL[...].astype(F32) + ZR[...].astype(F32))
     acc[...] = jnp.zeros_like(acc)
-    segment(0, 1)
+    segment(0, 3)
     for copy in (h0c, h0d, h0e, h0f):
         copy.wait_recv()
     for k in range(4):
-        Q[0, k] = R0[x, k, :, LO] + (RV[0, 0, k].astype(F32) + RV[0, 1, k].astype(F32))
+        Q[0, k] = fac[x, k, c, :, LO] + (RV[0, 0, k].astype(F32) + RV[0, 1, k].astype(F32))
     t0 = ring(0, "dp_1", y)
-    segment(1, 3)
+    segment(3, 5)
     for copy in (h1c, h1d, h1e, h1f):
         copy.wait_recv()
     for k in range(4):
-        Q[1, k] = R0[k, y, :, HI] + (RV[1, 0, k].astype(F32) + RV[1, 1, k].astype(F32))
+        Q[1, k] = fac[k, y, c, :, HI] + (RV[1, 0, k].astype(F32) + RV[1, 1, k].astype(F32))
     t1 = ring(1, "dp_0", x)
     u0 = ring_relay(0, "dp_1", t0)
-    segment(3, 5)
+    segment(5, 7)
     u1 = ring_relay(1, "dp_0", t1)
-    segment(5, 8)
-    total = acc[:, :128] + acc[:, 128:]
+    segment(7, 8)
+    total = acc[...]
     slots[...] = total.astype(BF16).reshape(128, 16, 128)
     few = jnp.sum((total * total).reshape(256, 8, 128), axis=0)
 
-    def send_slots(i, carry):
-        p = (me + i) % 128
+    def send_slots(p):
         pltpu.make_async_remote_copy(
             src_ref=slots.at[p], dst_ref=arrived_ref.at[me], send_sem=bulk.at[4],
-            recv_sem=bulk.at[5], device_id=place(p), device_id_type=MESH,
+            recv_sem=bulk.at[5], device_id=p, device_id_type=LOGICAL,
         ).start()
-        return carry
 
     for copy in u0 + u1:
         copy.wait_recv()
@@ -557,7 +592,7 @@
     grad_ref[:, HI] = upper
     GA[x, y, c, :, LO] = lower.astype(BF16)
     GA[x, y, c, :, HI] = upper.astype(BF16)
-    ga = Spread(GA, go_to, (x, y, c, z))
+    ga = Spread(GA, go_to, (x, y, c, z), ga_out, wsem.at[1])
     ga.first()
     both = lower * lower + upper * upper
     both = jnp.sum(both.reshape(4, 8, 1024), axis=0)
@@ -569,44 +604,38 @@
     bias_sum = jnp.sum(rv[...], axis=0)
     ns[...] = jnp.sum(few, axis=0, keepdims=True) + bias_sum * bias_sum
 
-    def send_norm(i, carry):
-        p = (me + i) % 128
+    def send_norm(p):
         pltpu.make_async_remote_copy(
             src_ref=ns, dst_ref=NR.at[me], send_sem=bulk.at[6],
-            recv_sem=bulk.at[7], device_id=place(p), device_id_type=MESH,
+            recv_sem=bulk.at[7], device_id=p, device_id_type=LOGICAL,
         ).start()
-        return carry
-
-    lax.fori_loop(1, 128, send_norm, 0)
-    lax.fori_loop(1, 128, send_slots, 0)
+
+    to_all(me, send_norm)
+    ga.second()
+    to_all(me, send_slots)
     NR[me] = ns[...]
     arrived_ref[me] = slots[me]
+    ga.third()
     aa.last()
-    put_aa = pltpu.make_async_copy(AA, aa_out, local.at[2])
-    put_aa.start()
-    ga.second()
-    ga.third()
-    ga.fourth()
     lot = NR.at[pl.ds(0, 127)]
     pltpu.make_async_copy(lot, lot, bulk.at[7]).wait()
     lanes = jnp.sum(NR[...], axis=0)
     norm = jnp.sum(lanes, axis=1, keepdims=True)
     scale = clip_norm / jnp.maximum(jnp.sqrt(norm), clip_norm)
     scale_ref[...] = jnp.broadcast_to(scale, (8, 128))
+    ga.fourth()
     ga.fifth()
     many = arrived_ref.at[pl.ds(0, 127)]
     pltpu.make_async_copy(many, many, bulk.at[5]).wait()
     ga.last()
-    put_ga = pltpu.make_async_copy(GA, ga_out, local.at[3])
-    put_ga.start()
     pltpu.make_async_copy(lot, lot, bulk.at[6]).wait()
     pltpu.make_async_copy(many, many, bulk.at[4]).wait()
     lot = idsend.at[pl.ds(0, 127)]
     pltpu.make_async_copy(lot, lot, bulk.at[0]).wait()
     pltpu.make_async_copy(lot, lot, bulk.at[1]).wait()
     cp.drain()
-    put_aa.wait()
-    put_ga.wait()
+    aa.close()
+    ga.close()
 
 
 def finish_kernel(
@@ -617,13 +646,11 @@
 ):
     chunk = 128
     count = 1024 // chunk
-    loads = []
     for i in range(count):
         rows = pl.ds(i * chunk, chunk)
         for j, (src, dst) in enumerate(((ga_any, GA), (aa_any, AA), (w_any, W))):
             copy = pltpu.make_async_copy(src.at[rows], dst.at[rows], sem.at[i, j])
             copy.start()
-            loads.append(copy)
     scale = scale_ref[0:1, 0:1]
     clipped = scale * grad_ref[...]
     dense_new_ref[...] = dense_ref[...] + clipped * clipped
@@ -656,9 +683,19 @@
             same = jnp.where((lane < 64) == (side == 0), block, turned)
             values.append(jnp.where((lane >= 64) == (high > 0.5), same, 0.0).astype(BF16))
         acc[...] += mm(jnp.concatenate(hots, axis=1), jnp.concatenate(values, axis=0), 1, 0)
+        rows = pl.ds(pl.multiple_of(t * chunk, chunk), chunk)
+        for j, (src, dst) in enumerate(((ga_any, GA), (aa_any, AA), (w_any, W))):
+            pltpu.make_async_copy(src.at[rows], dst.at[rows], sem.at[t, j]).wait()
+        for q in range(16):
+            cols = slice(128 * q, 128 * q + 128)
+            g = scale * GA[rows, cols].astype(F32)
+            r = lax.rsqrt(AA[rows, cols].astype(F32) + g * g)
+            r = r - (adagrad_eps * r) * r
+            WN[rows, cols] = (W[rows, cols].astype(F32) - (dense_rate * g) * r).astype(BF16)
+        pltpu.make_async_copy(WN.at[rows], wn_any.at[rows], osem).start()
         return carry
 
-    lax.fori_loop(0, arrived_ref.shape[0] // step, part, 0)
+    lax.fori_loop(0, count, part, 0)
     for p in range(pairs // 128):
         both = acc[128 * p : 128 * p + 128, :].T * scale
         for upper in range(2):
@@ -667,30 +704,9 @@
             fresh = accum_ref[line : line + 1, :] + jnp.sum(r * r, axis=0, keepdims=True) / 64.0
             accum_new_ref[line : line + 1, :] = fresh
             at = line * 128
-            new_ref[:, at : at + 128] = table_ref[:, at : at + 128] - table_rate * r / (
-                jnp.sqrt(fresh) + adagrad_eps
-            )
-
-    for copy in loads:
-        copy.wait()
-
-    def weights(i, carry):
-        rows = pl.ds(pl.multiple_of(i * chunk, chunk), chunk)
-
-        def tile(t, carry):
-            cols = pl.ds(pl.multiple_of(t * 512, 512), 512)
-            g = scale * GA[rows, cols].astype(F32)
-            fresh = AA[rows, cols].astype(F32) + g * g
-            WN[rows, cols] = (
-                W[rows, cols].astype(F32) - dense_rate * g / (jnp.sqrt(fresh) + adagrad_eps)
-            ).astype(BF16)
-            return carry
-
-        lax.fori_loop(0, 4, tile, 0)
-        pltpu.make_async_copy(WN.at[rows], wn_any.at[rows], osem).start()
-        return carry
-
-    lax.fori_loop(0, count, weights, 0)
+            rate = table_rate / (jnp.sqrt(fresh) + adagrad_eps)
+            new_ref[:, at : at + 128] = table_ref[:, at : at + 128] - r * rate
+
     pltpu.make_async_copy(WN, wn_any, osem).wait()
 
 
@@ -732,12 +748,13 @@
             V((3, 256, 1024), BF16), V((2, 128, 1024), F32),
             V((128, 1024), BF16), V((128, 1024), BF16),
             V((256, 1024), BF16), V((256, 1024), BF16), V((256, 1024), F32),
-            V((4, 4, 32, 2048), F32), V((4, 4, 32, 2048), BF16),
+            V((4, 4, 32, 2048), BF16), V((4, 4, 32, 2048), BF16),
             V((2, 2, 2, 32, 1024), BF16), V((2, 2, 4, 32, 1024), BF16),
             V((2, 4, 32, 1024), F32), V((2, 2, 16, 1024), F32), V((2, 2, 32, 1024), F32),
-            V(whole, BF16), V(whole, BF16), V((2048, 256), F32), V((128, 16, 128), BF16),
-            V((1, 128), F32), V((128, 1, 128), F32),
-            DMA((N_COPIES,)), DMA((N_COPIES,)), DMA((8,)), DMA((4,)),
+            V(whole, BF16), V(whole, BF16), V((2048, 128), F32), V((128, 16, 128), BF16),
+            V((1, 128), F32), V((128, 1, 128), F32), V((4, 4, 32, 2048), BF16),
+            V((2048, 128), BF16), V((1, 2048), F32),
+            DMA((N_COPIES,)), DMA((N_COPIES,)), DMA((8,)), DMA((2,)), DMA((2, 16)),
         ],
         compiler_params=pltpu.CompilerParams(
             has_side_effects=True, vmem_limit_bytes=63 * 1024 * 1024, collective_id=0
@@ -746,12 +763,12 @@
     )(
         lookup_slots.T,
         peer_counts,
-        slab_values[0].reshape(2048, 128),
+        slab_values[0],
         row_ids[0].T,
         labels.reshape(8, 128),
         sample_weight.reshape(8, 128),
         bias_in.reshape(1, 2048),
-        weight_out.astype(F32).reshape(1, 2048),
+        weight_out.reshape(16, 128),
         weight_in,
         dense_accum,
     )

time: 141 us -> 119 us (0.84)
  Pallas kernels: 136 us -> 118 us
  local copies, waits for them, and re-layouts: 2.07 us -> 0 us
    pallas_call x1, Pallas kernels: 120 us -> 103 us  [body(): pl.pallas_call(step_kernel, out_shape=(shape(whole, BF16), shape(whole, B...]
    another operation x1 -> x0, local copies, waits for them, and re-layouts: 2.07 us -> none  [body(): slab_values[0].reshape(2048, 128)]
    pallas_call x1, Pallas kernels: 16.6 us -> 15 us  [body(): pl.pallas_call(finish_kernel, out_shape=(shape((64, 4096), F32), shape((3...]
where the time goes in v3:
time: 119 us
  Pallas kernels  118 us (99%)
    pallas_call x1, Pallas kernels, body(): pl.pallas_call(step_kernel, out_shape=(shape(whole, BF16), shape(whole, B...  103 us
    pallas_call x1, Pallas kernels, body(): pl.pallas_call(finish_kernel, out_shape=(shape((64, 4096), F32), shape((3...  15 us

profile of v3, /device:TPU:1, one launch (start us, length us, event | category | flops | bytes accessed | tf_op | source)
XLA Modules:
  0.0 119.0 jit_solution(14429649687170521634)
XLA Ops:
  0.6 103.1 %step.1 = (bf16[4,4,2,32,2048]{4,3,2,1,0:T(8,128)(2,1)}, bf16[4,4,2,32,2048]{4,3,2,1,0:T(8,128)(2,1)}, bf16[128,16,128]{2,1,0:T(8,128)(2,1)}, s32[128,1,128]{2,1...) custom-call(s32[16,256]{1,0:T(8,128)} %bitcast.23, s32[1,128]{1,0:T(1,128)} %counts_ref.1, bf16[128,2048]{1,0:T(8,128)(2,1)} %bitcast.20, ...), custom_call_target="tpu_custom_call" | custom-call | tf_op jit(solution)/shard_map/step/pallas_call | solution.py:734
  103.8 15.0 %finish.1 = (f32[64,4096]{1,0:T(8,128)}, f32[32,128]{1,0:T(8,128)}, f32[32,2048]{1,0:T(8,128)}, bf16[1024,2048]{1,0:T(8,128)(2,1)}) custom-call(bf16[2048,128]{1,0:T(8,128)(2,1)} %bitcast.21, s32[16,8,128]{2,1,0:T(8,128)} %bitcast.22, f32[8,128]{1,0:T(8,128)} %get-tuple-element.16.scale_ref, f32[64,4096]{1,0:T(8,128)} %bitcast.19, f32[32,128]{1,0:T(8,128)} %bitcast.25, ...), custom_call_target="tpu_custom_call" | custom-call | tf_op jit(solution)/shard_map/finish/pallas_call | solution.py:775

commit v4 on v3

--- a/solution.py
+++ b/solution.py
@@ -37,9 +37,10 @@
     return tuple(lax.axis_index(a) for a in DP_MP)
 
 
-def to_all(me, emit):
-    for u in range(1, 8):
-        emit(lax.rem(me + u, 128))
+def to_all(me, emit, first=0, last=16):
+    if first == 0:
+        for u in range(1, 8):
+            emit(lax.rem(me + u, 128))
 
     def more(j, carry):
         base = me + 8 * j
@@ -47,7 +48,7 @@
             emit(lax.rem(base + u, 128))
         return carry
 
-    lax.fori_loop(1, 16, more, 0)
+    lax.fori_loop(max(first, 1), last, more, 0)
 
 
 class Copies:
@@ -229,13 +230,15 @@
 
 
 def step_kernel(
+    lookups_any, counts_any, slab_any, ids_any, label_any, sw_any, bias_any, wout_any,
+    w_any, accum_any,
+    ga_out, aa_out, sums_out, scale_out, grad_out,
     lookups_ref, counts_ref, slab_ref, ids_ref, label_ref, sw_ref, bias_ref, wout_ref,
-    w_any, accum_any,
-    ga_out, aa_out, arrived_ref, rids_ref, scale_ref, grad_ref,
+    arrived_ref, rids_ref, scale_ref, grad_ref, lined,
     W, A, idsend, G, fac, hidden, dact, pacc, lg, LR, DL, gb, go, sv, rv,
     ZS, Df, ZRL, ZRR, ZL, ZR, DPL,
     R0, SB, RL, RV, Q, RL2, RV2,
-    GA, AA, acc, slots, ns, NR, SC, slab, wout,
+    GA, AA, acc, slots, ns, NR, SC, slab, wout, strided,
     ssem, rsem, bulk, local, wsem,
 ):
     x, y, c, z = position()
@@ -248,17 +251,22 @@
     yr, yl, yo = (y + 1) % 4, (y + 3) % 4, (y + 2) % 4
     LO, HI = slice(0, 1024), slice(1024, 2048)
 
+    pairs_of = (
+        (counts_any, counts_ref), (lookups_any, lookups_ref), (slab_any, slab_ref),
+        (wout_any, wout_ref), (accum_any, A), (bias_any, bias_ref), (ids_any, ids_ref),
+        (label_any, label_ref), (sw_any, sw_ref), (w_any, W),
+    )
+    loads = [pltpu.make_async_copy(a, b, local.at[k]) for k, (a, b) in enumerate(pairs_of)]
+    for copy in loads:
+        copy.start()
     barrier = pltpu.get_barrier_semaphore()
 
     def greet(p):
         pl.semaphore_signal(barrier, inc=1, device_id=p, device_id_type=LOGICAL)
 
     to_all(me, greet)
-    fetch_a = pltpu.make_async_copy(accum_any, A, local.at[1])
-    fetch_a.start()
-    fetch_w = pltpu.make_async_copy(w_any, W, local.at[0])
-    fetch_w.start()
-
+    for copy in loads[:5]:
+        copy.wait()
     starts, ends = owner_bounds(counts_ref)
     own_rows = pl.ds(pl.multiple_of(z * 256, 256), 256)
 
@@ -291,13 +299,12 @@
         left[k] = go_to(block(z, k), block(z, k), {"mp": zl})
 
     for k in range(16):
-        acc[pl.ds(k, 128, stride=16), :] = slab_ref[:, k * 128 : k * 128 + 128].astype(F32)
-    slab[...] = acc[...].astype(BF16)
+        strided[pl.ds(k, 128, stride=16), :] = slab_ref[:, k * 128 : k * 128 + 128].astype(F32)
+    slab[...] = strided[...].astype(BF16)
     for k in range(16):
         wout[:, k * 128 : k * 128 + 128] = wout_ref[k : k + 1, :].astype(F32)
     gather_pair(0)
     gather_pair(1)
-    fetch_a.wait()
     AA[x, y, c] = A[...].astype(BF16)
     pl.semaphore_wait(barrier, 127)
     send_block(0)
@@ -312,11 +319,13 @@
     gather_pair(6)
     gather_pair(7)
     send_block(3)
+    for copy in loads[5:9]:
+        copy.wait()
     turned = jnp.concatenate([ids_ref[...].astype(F32), jnp.zeros((96, 128), F32)], axis=0)
     idsend[...] = turned.T.astype(I32).reshape(128, 1, 128)
     to_all(me, send_ids)
     rids_ref[me] = idsend[me]
-    fetch_w.wait()
+    loads[9].wait()
 
     def forward(src):
         rows = pl.ds(pl.multiple_of(src * 256, 256), 256)
@@ -334,7 +343,7 @@
             pacc[...] += (m[:, 0:128] + m[:, 128:256]) + (m[:, 256:384] + m[:, 384:512])
             return carry
 
-        lax.fori_loop(0, 4, tile, 0)
+        lax.fori_loop(0, 4, tile, 0, unroll=2)
         for s in range(2):
             line = jnp.sum(pacc[128 * s : 128 * s + 128, :].T, axis=0, keepdims=True)
             lg[pl.ds(src * 2 + s, 1), :] = line
@@ -416,13 +425,13 @@
         at = pl.multiple_of(xi * 256, 256)
 
         def tile(t, carry):
-            cols = pl.ds(pl.multiple_of(t * 512, 512), 512)
+            cols = pl.ds(pl.multiple_of(t * 1024, 1024), 1024)
             g = mm(G[:, pl.ds(at, 256)], dact[:, cols], 0, 0)
-            fac[xi, :, :, :, cols] = g.reshape(4, 2, 32, 512)
+            fac[xi, :, :, :, cols] = g.reshape(4, 2, 32, 1024)
             SC[xi, :, :, cols] = fac[xi, :, 1 - c, :, cols].astype(BF16)
             return carry
 
-        lax.fori_loop(0, 4, tile, 0)
+        lax.fori_loop(0, 2, tile, 0)
         to_core[tag] = go_to(SC.at[xi], R0.at[xi], partner)
 
     def chip_sum(xi, tag):
@@ -441,16 +450,15 @@
         Df[1, :, cols] = d[128:256]
 
     weight_grad(xo, "o")
-    aa.fourth()
-    weight_grad(xr, "r")
     dpool(zr, put_right)
     z3 = go_to(ZS.at[1, 128:256], ZL.at[128:256], {"mp": zr})
+    dpool(zl, put_left)
+    z4 = go_to(ZS.at[2, 0:128], ZR.at[0:128], {"mp": zl})
     chip_sum(xo, "o")
     h0a = go_to(SB.at[xo, 0:2, :, LO], RL.at[0, 0], {"dp_0": xr})
     h0b = go_to(SB.at[xo, 2:4, :, LO], RL.at[0, 1], {"dp_0": xl})
+    weight_grad(xr, "r")
     weight_grad(xl, "l")
-    dpool(zl, put_left)
-    z4 = go_to(ZS.at[2, 0:128], ZR.at[0:128], {"mp": zl})
     chip_sum(xr, "r")
     h0c = go_to(SB.at[xr, 2:4, :, LO], RV.at[0, 0, 2:4], {"dp_0": xr})
     weight_grad(x, "m")
@@ -462,6 +470,12 @@
     z2.wait_recv()
     ZS[2, 128:256, :] = (Df[1] + ZRR[...].astype(F32)).astype(BF16)
     z6 = go_to(ZS.at[2, 128:256], ZR.at[128:256], {"mp": zl})
+    aa.fourth()
+
+    def put_own(d, cols):
+        DPL[:, cols] = d
+
+    dpool(z, put_own)
     chip_sum(x, "m")
     h1a = go_to(SB.at[0:2, yo, :, HI], RL.at[1, 0], {"dp_1": yr})
     h1b = go_to(SB.at[2:4, yo, :, HI], RL.at[1, 1], {"dp_1": yl})
@@ -497,10 +511,6 @@
     lax.fori_loop(1, 32, send_small, 0)
     rv[dp] = sv[dp]
 
-    def put_own(d, cols):
-        DPL[:, cols] = d
-
-    dpool(z, put_own)
     h1a.wait_recv()
     for k in range(2):
         SB[k, yr, :, HI] = (fac[k, yr, c, :, HI] + RL[1, 0, k].astype(F32)).astype(BF16)
@@ -537,52 +547,75 @@
             hots, rows = [], []
             for side in range(2):
                 slot = slot_rows(lookups_ref[pl.ds(2 * k + side, 1), :], starts, ends)
-                low = slot - 16.0 * jnp.floor(slot * (1.0 / 16.0))
-                upper = jnp.floor(slot * (1.0 / 16.0)) - 2.0 * jnp.floor(slot * (1.0 / 32.0))
-                hots.append(
-                    tiles_over_rows(16.0 * jnp.floor(slot * (1.0 / 32.0)) + low, 128)
-                )
-                upper = as_column(upper)
+                slot = as_column(slot)
+                sixteen = jnp.floor(slot * (1.0 / 16.0))
+                both = jnp.floor(slot * (1.0 / 32.0))
+                upper = sixteen - 2.0 * both
+                hots.append(tiles_over_lanes(slot - 16.0 * (sixteen - both), 16))
                 same = jnp.where((lane < 64) == (side == 0), block, turned)
                 kept = jnp.where((lane >= 64) == (upper > 0.5), same, 0.0)
-                high = kept.astype(BF16)
-                rest = (kept - high.astype(F32)).astype(BF16)
-                rows.append(jnp.concatenate([high, rest], axis=1))
-            part = mm(jnp.concatenate(hots, axis=1), jnp.concatenate(rows, axis=0), 1, 0)
-            acc[...] += part[:, :128] + part[:, 128:]
+                rows.append(kept.astype(BF16))
+            acc[...] += mm(jnp.concatenate(rows, axis=0), jnp.concatenate(hots, axis=0), 0, 0)
             return carry
 
         lax.fori_loop(first, last, pair, 0)
+
+    def rows_of_table(first, last):
+        def part(t, carry):
+            lane = iota((256, 128), 1)
+            block = arrived_ref[pl.ds(16 * t, 16)].reshape(256, 128).astype(F32)
+            turned = pltpu.roll(block, 64, 1)
+            hots, values = [], []
+            for side in range(2):
+                row = jnp.concatenate(
+                    [lined[side, pl.ds(2 * t, 1), :], lined[side, pl.ds(2 * t + 1, 1), :]], axis=1
+                )
+                row = as_column(row)
+                above = row >= 2048.0
+                hots.append(tiles_over_lanes(jnp.where(above, row - 2048.0, row), 16))
+                same = jnp.where((lane < 64) == (side == 0), block, turned)
+                values.append(jnp.where((lane >= 64) == above, same, 0.0).astype(BF16))
+            acc[...] += mm(
+                jnp.concatenate(values, axis=0), jnp.concatenate(hots, axis=0), 0, 0
+            )
+            return carry
+
+        lax.fori_loop(first, last, part, 0)
 
     for copy in (z3, z4, z5, z6):
         copy.wait_recv()
     DPL[...] = DPL[...] + (ZL[...].astype(F32) + ZR[...].astype(F32))
     acc[...] = jnp.zeros_like(acc)
-    segment(0, 3)
+    segment(0, 2)
     for copy in (h0c, h0d, h0e, h0f):
         copy.wait_recv()
     for k in range(4):
         Q[0, k] = fac[x, k, c, :, LO] + (RV[0, 0, k].astype(F32) + RV[0, 1, k].astype(F32))
     t0 = ring(0, "dp_1", y)
-    segment(3, 5)
+    segment(2, 4)
     for copy in (h1c, h1d, h1e, h1f):
         copy.wait_recv()
     for k in range(4):
         Q[1, k] = fac[k, y, c, :, HI] + (RV[1, 0, k].astype(F32) + RV[1, 1, k].astype(F32))
     t1 = ring(1, "dp_0", x)
     u0 = ring_relay(0, "dp_1", t0)
-    segment(5, 7)
+    segment(4, 6)
     u1 = ring_relay(1, "dp_0", t1)
-    segment(7, 8)
-    total = acc[...]
-    slots[...] = total.astype(BF16).reshape(128, 16, 128)
-    few = jnp.sum((total * total).reshape(256, 8, 128), axis=0)
+    segment(6, 8)
+    few = jnp.zeros((8, 128), F32)
+    for t in range(16):
+        piece = acc[:, 128 * t : 128 * t + 128]
+        few = few + jnp.sum((piece * piece).reshape(16, 8, 128), axis=0)
+        slots[8 * t : 8 * t + 8] = piece.T.astype(BF16).reshape(8, 16, 128)
 
     def send_slots(p):
         pltpu.make_async_remote_copy(
             src_ref=slots.at[p], dst_ref=arrived_ref.at[me], send_sem=bulk.at[4],
             recv_sem=bulk.at[5], device_id=p, device_id_type=LOGICAL,
         ).start()
+
+    to_all(me, send_slots)
+    arrived_ref[me] = slots[me]
 
     for copy in u0 + u1:
         copy.wait_recv()
@@ -611,78 +644,84 @@
         ).start()
 
     to_all(me, send_norm)
+    put_grad = pltpu.make_async_copy(grad_ref, grad_out, local.at[10])
+    put_grad.start()
+    NR[me] = ns[...]
     ga.second()
-    to_all(me, send_slots)
-    NR[me] = ns[...]
-    arrived_ref[me] = slots[me]
+
+    heard = idsend.at[pl.ds(0, 127)]
+    pltpu.make_async_copy(heard, heard, bulk.at[1]).wait()
+    lane16 = iota((16, 128), 1) // 16
+    numbers = rids_ref[...].astype(F32).reshape(16, 8, 128)
+    for side in range(2):
+        line = jnp.zeros((16, 128), F32)
+        for d in range(8):
+            shift = (16 * d - 16 * side) % 128
+            line = jnp.where(lane16 == d, pltpu.roll(numbers[:, d, :], shift, 1), line)
+        lined[side] = line
+    acc[...] = jnp.zeros_like(acc)
+    aa.last()
     ga.third()
-    aa.last()
+    many = arrived_ref.at[pl.ds(0, 127)]
+    pltpu.make_async_copy(many, many, bulk.at[5]).wait()
+    rows_of_table(0, 5)
+    ga.fourth()
+    rows_of_table(5, 8)
+    put_sums = pltpu.make_async_copy(acc, sums_out, local.at[11])
+    put_sums.start()
     lot = NR.at[pl.ds(0, 127)]
     pltpu.make_async_copy(lot, lot, bulk.at[7]).wait()
     lanes = jnp.sum(NR[...], axis=0)
     norm = jnp.sum(lanes, axis=1, keepdims=True)
     scale = clip_norm / jnp.maximum(jnp.sqrt(norm), clip_norm)
     scale_ref[...] = jnp.broadcast_to(scale, (8, 128))
-    ga.fourth()
+    put_scale = pltpu.make_async_copy(scale_ref, scale_out, local.at[12])
+    put_scale.start()
     ga.fifth()
-    many = arrived_ref.at[pl.ds(0, 127)]
-    pltpu.make_async_copy(many, many, bulk.at[5]).wait()
     ga.last()
     pltpu.make_async_copy(lot, lot, bulk.at[6]).wait()
     pltpu.make_async_copy(many, many, bulk.at[4]).wait()
-    lot = idsend.at[pl.ds(0, 127)]
-    pltpu.make_async_copy(lot, lot, bulk.at[0]).wait()
-    pltpu.make_async_copy(lot, lot, bulk.at[1]).wait()
+    pltpu.make_async_copy(heard, heard, bulk.at[0]).wait()
+    put_grad.wait()
+    put_sums.wait()
+    put_scale.wait()
     cp.drain()
     aa.close()
     ga.close()
 
 
 def finish_kernel(
-    arrived_ref, rids_ref, scale_ref, table_ref, accum_ref, grad_ref, dense_ref,
+    sums_any, scale_ref, table_any, accum_any, grad_any, dense_any,
     ga_any, aa_any, w_any,
-    new_ref, accum_new_ref, dense_new_ref, wn_any,
-    acc, ids, GA, AA, W, WN, sem, osem,
+    new_any, accum_new_any, dense_new_any, wn_any,
+    GA, AA, W, WN, sums, table, accum, grad, dense, new, accum_new, dense_new, sem, isem, osem,
 ):
     chunk = 128
     count = 1024 // chunk
-    for i in range(count):
+
+    def load(i):
         rows = pl.ds(i * chunk, chunk)
         for j, (src, dst) in enumerate(((ga_any, GA), (aa_any, AA), (w_any, W))):
-            copy = pltpu.make_async_copy(src.at[rows], dst.at[rows], sem.at[i, j])
-            copy.start()
+            pltpu.make_async_copy(src.at[rows], dst.at[rows], sem.at[i, j]).start()
+
+    small = [
+        pltpu.make_async_copy(src, dst, isem.at[k])
+        for k, (src, dst) in enumerate(
+            (
+                (grad_any, grad), (dense_any, dense), (accum_any, accum),
+                (sums_any, sums), (table_any, table),
+            )
+        )
+    ]
+    load(0)
+    load(1)
+    for copy in small:
+        copy.start()
+    for i in range(2, count):
+        load(i)
     scale = scale_ref[0:1, 0:1]
-    clipped = scale * grad_ref[...]
-    dense_new_ref[...] = dense_ref[...] + clipped * clipped
-
-    lane16 = iota((16, 128), 1) // 16
-    for upper in range(2):
-        lined = jnp.zeros((16, 128), F32)
-        for d in range(8):
-            piece = rids_ref[:, d, :].astype(F32)
-            lined = jnp.where(lane16 == d, pltpu.roll(piece, (16 * d - 16 * upper) % 128, 1), lined)
-        ids[upper] = lined
-
-    pairs = acc.shape[0]
-    acc[...] = jnp.zeros_like(acc)
-    step = 256
 
     def part(t, carry):
-        lane = iota((step, 128), 1)
-        base = pl.multiple_of(t * step, step)
-        block = arrived_ref[pl.ds(base, step), :].astype(F32)
-        turned = pltpu.roll(block, 64, 1)
-        hots, values = [], []
-        for side in range(2):
-            row = jnp.concatenate(
-                [ids[side, pl.ds(2 * t, 1), :], ids[side, pl.ds(2 * t + 1, 1), :]], axis=1
-            )
-            above = row >= float(pairs)
-            hots.append(tiles_over_rows(jnp.where(above, row - float(pairs), row), pairs // 16))
-            high = as_column(jnp.where(above, 1.0, 0.0))
-            same = jnp.where((lane < 64) == (side == 0), block, turned)
-            values.append(jnp.where((lane >= 64) == (high > 0.5), same, 0.0).astype(BF16))
-        acc[...] += mm(jnp.concatenate(hots, axis=1), jnp.concatenate(values, axis=0), 1, 0)
         rows = pl.ds(pl.multiple_of(t * chunk, chunk), chunk)
         for j, (src, dst) in enumerate(((ga_any, GA), (aa_any, AA), (w_any, W))):
             pltpu.make_async_copy(src.at[rows], dst.at[rows], sem.at[t, j]).wait()
@@ -692,22 +731,35 @@
             r = lax.rsqrt(AA[rows, cols].astype(F32) + g * g)
             r = r - (adagrad_eps * r) * r
             WN[rows, cols] = (W[rows, cols].astype(F32) - (dense_rate * g) * r).astype(BF16)
-        pltpu.make_async_copy(WN.at[rows], wn_any.at[rows], osem).start()
+        pltpu.make_async_copy(WN.at[rows], wn_any.at[rows], osem.at[0]).start()
         return carry
 
     lax.fori_loop(0, count, part, 0)
-    for p in range(pairs // 128):
-        both = acc[128 * p : 128 * p + 128, :].T * scale
-        for upper in range(2):
-            r = both[64 * upper : 64 * upper + 64, :]
-            line = p + upper * (pairs // 128)
-            fresh = accum_ref[line : line + 1, :] + jnp.sum(r * r, axis=0, keepdims=True) / 64.0
-            accum_new_ref[line : line + 1, :] = fresh
+    for copy in small:
+        copy.wait()
+    clipped = scale * grad[...]
+    dense_new[...] = dense[...] + clipped * clipped
+    puts = [pltpu.make_async_copy(dense_new, dense_new_any, osem.at[1])]
+    puts[0].start()
+    for upper in range(2):
+        for p in range(16):
+            r = sums[64 * upper : 64 * upper + 64, 128 * p : 128 * p + 128] * scale
+            line = p + upper * 16
+            fresh = accum[line : line + 1, :] + jnp.sum(r * r, axis=0, keepdims=True) / 64.0
+            accum_new[line : line + 1, :] = fresh
             at = line * 128
             rate = table_rate / (jnp.sqrt(fresh) + adagrad_eps)
-            new_ref[:, at : at + 128] = table_ref[:, at : at + 128] - r * rate
-
-    pltpu.make_async_copy(WN, wn_any, osem).wait()
+            new[:, at : at + 128] = table[:, at : at + 128] - r * rate
+        cols = pl.ds(2048 * upper, 2048)
+        puts.append(
+            pltpu.make_async_copy(new.at[:, cols], new_any.at[:, cols], osem.at[2 + upper])
+        )
+        puts[-1].start()
+    puts.append(pltpu.make_async_copy(accum_new, accum_new_any, osem.at[4]))
+    puts[-1].start()
+    pltpu.make_async_copy(WN, wn_any, osem.at[0]).wait()
+    for copy in puts:
+        copy.wait()
 
 
 def shape(dims, kind):
@@ -731,15 +783,19 @@
     V = pltpu.VMEM
     DMA = pltpu.SemaphoreType.DMA
     whole = (4, 4, 2, 32, 2048)
-    ga, aa, arrived, rids, scale, grad = pl.pallas_call(
+    ga, aa, sums, scale, grad = pl.pallas_call(
         step_kernel,
         out_shape=(
-            shape(whole, BF16), shape(whole, BF16), shape((128, 16, 128), BF16),
-            shape((128, 1, 128), I32), shape((8, 128), F32), shape((32, 2048), F32),
+            shape(whole, BF16), shape(whole, BF16), shape((128, 2048), F32),
+            shape((8, 128), F32), shape((32, 2048), F32),
         ),
-        in_specs=[VM] * 8 + [ANY] * 2,
-        out_specs=(ANY, ANY, VM, VM, VM, VM),
+        in_specs=[ANY] * 10,
+        out_specs=(ANY,) * 5,
         scratch_shapes=[
+            V((16, 256), I32), V((1, 128), I32), V((128, 2048), BF16), V((32, 128), I32),
+            V((8, 128), I32), V((8, 128), F32), V((1, 2048), F32), V((16, 128), BF16),
+            V((128, 16, 128), BF16), V((128, 1, 128), I32), V((8, 128), F32), V((32, 2048), F32),
+            V((2, 16, 128), F32),
             V((1024, 2048), BF16), V((32, 2048), F32), V((128, 1, 128), I32),
             V((1024, 1024), BF16), V(whole, F32), V((1024, 2048), BF16),
             V((1024, 2048), BF16), V((256, 128), F32), V((8, 128), F32), V((4, 8, 128), F32),
@@ -751,10 +807,10 @@
             V((4, 4, 32, 2048), BF16), V((4, 4, 32, 2048), BF16),
             V((2, 2, 2, 32, 1024), BF16), V((2, 2, 4, 32, 1024), BF16),
             V((2, 4, 32, 1024), F32), V((2, 2, 16, 1024), F32), V((2, 2, 32, 1024), F32),
-            V(whole, BF16), V(whole, BF16), V((2048, 128), F32), V((128, 16, 128), BF16),
+            V(whole, BF16), V(whole, BF16), V((128, 2048), F32), V((128, 16, 128), BF16),
             V((1, 128), F32), V((128, 1, 128), F32), V((4, 4, 32, 2048), BF16),
-            V((2048, 128), BF16), V((1, 2048), F32),
-            DMA((N_COPIES,)), DMA((N_COPIES,)), DMA((8,)), DMA((2,)), DMA((2, 16)),
+            V((2048, 128), BF16), V((1, 2048), F32), V((2048, 128), F32),
+            DMA((N_COPIES,)), DMA((N_COPIES,)), DMA((8,)), DMA((13,)), DMA((2, 16)),
         ],
         compiler_params=pltpu.CompilerParams(
             has_side_effects=True, vmem_limit_bytes=63 * 1024 * 1024, collective_id=0
@@ -778,17 +834,17 @@
             shape((64, 4096), F32), shape((32, 128), F32), shape((32, 2048), F32),
             shape((1024, 2048), BF16),
         ),
-        in_specs=[VM] * 7 + [ANY] * 3,
-        out_specs=(VM, VM, VM, ANY),
+        in_specs=[ANY, VM] + [ANY] * 7,
+        out_specs=(ANY,) * 4,
         scratch_shapes=[
-            V((2048, 128), F32), V((2, 16, 128), F32),
             V((1024, 2048), BF16), V((1024, 2048), BF16), V((1024, 2048), BF16),
-            V((1024, 2048), BF16), DMA((8, 3)), DMA,
+            V((1024, 2048), BF16), V((128, 2048), F32), V((64, 4096), F32), V((32, 128), F32),
+            V((32, 2048), F32), V((32, 2048), F32), V((64, 4096), F32), V((32, 128), F32),
+            V((32, 2048), F32), DMA((8, 3)), DMA((5,)), DMA((5,)),
         ],
         name="finish",
     )(
-        arrived.reshape(2048, 128),
-        rids.reshape(16, 8, 128),
+        sums,
         scale,
         table_rows.T,
         table_accum.reshape(32, 128),

time: 119 us -> 109 us (0.916)
  Pallas kernels: 118 us -> 108 us
    pallas_call x1, Pallas kernels: 15 us -> 9.22 us  [body(): pl.pallas_call(finish_kernel, out_shape=(shape((64, 4096), F32), shape((3...]
    pallas_call x1, Pallas kernels: 103 us -> 98.5 us  [body(): pl.pallas_call(step_kernel, out_shape=(shape(whole, BF16), shape(whole, B...]
where the time goes in v4:
time: 109 us; the launch traced here: 108 us
  Pallas kernels  108 us (99%)
    pallas_call x1, Pallas kernels, body(): pl.pallas_call(step_kernel, out_shape=(shape(whole, BF16), shape(whole, B...  98.5 us
    pallas_call x1, Pallas kernels, body(): pl.pallas_call(finish_kernel, out_shape=(shape((64, 4096), F32), shape((3...  9.22 us

profile of v4, /device:TPU:1, one launch (start us, length us, event | category | flops | bytes accessed | tf_op | source)
XLA Modules:
  0.0 108.5 jit_solution(17908575250531539977)
XLA Ops:
  0.6 98.5 %step.1 = (bf16[4,4,2,32,2048]{4,3,2,1,0:T(8,128)(2,1)}, bf16[4,4,2,32,2048]{4,3,2,1,0:T(8,128)(2,1)}, f32[128,2048]{1,0:T(8,128)}, f32[8,128]{1,0:T(8,128)}, f32[32,2048]{1,0:T(8,128)}) custom-call(s32[16,256]{1,0:T(8,128)} %bitcast.19, s32[1,128]{1,0:T(1,128)} %counts_any.1, bf16[128,2048]{1,0:T(8,128)(2,1)} %bitcast.18, s32[32,128]{1,0:T(8,128)} %bitcast.20, ...), custom_call_target="tpu_custom_call" | custom-call | tf_op jit(solution)/shard_map/step/pallas_call | solution.py:786
  99.1 9.2 %finish.1 = (f32[64,4096]{1,0:T(8,128)}, f32[32,128]{1,0:T(8,128)}, f32[32,2048]{1,0:T(8,128)}, bf16[1024,2048]{1,0:T(8,128)(2,1)}) custom-call(f32[128,2048]{1,0:T(8,128)} %get-tuple-element.13.sums_any, f32[8,128]{1,0:T(8,128)} %get-tuple-element.14.scale_ref, f32[64,4096]{1,0:T(8,128)} %bitcast.17, f32[32,128]{1,0:T(8,128)} %bitcast.21, ...), custom_call_target="tpu_custom_call" | custom-call | tf_op jit(solution)/shard_map/finish/pallas_call | solution.py:831

commit v5 on v4

--- a/solution.py
+++ b/solution.py
@@ -37,10 +37,9 @@
     return tuple(lax.axis_index(a) for a in DP_MP)
 
 
-def to_all(me, emit, first=0, last=16):
-    if first == 0:
-        for u in range(1, 8):
-            emit(lax.rem(me + u, 128))
+def to_all(me, emit):
+    for u in range(1, 8):
+        emit(lax.rem(me + u, 128))
 
     def more(j, carry):
         base = me + 8 * j
@@ -48,31 +47,36 @@
             emit(lax.rem(base + u, 128))
         return carry
 
-    lax.fori_loop(max(first, 1), last, more, 0)
+    lax.fori_loop(1, 16, more, 0)
 
 
 class Copies:
     def __init__(self, send, recv):
-        self.send, self.recv, self.used, self.open = send, recv, 0, []
-
-    def go(self, src, dst, where):
-        k = self.used
-        self.used += 1
+        self.send, self.recv, self.used, self.sent = send, recv, 0, [0]
+
+    def go(self, src, dst, where, send=None):
+        if send is None:
+            rows = src.size * (4 if src.dtype == F32 else 2) // 4096
+            if self.sent[-1] + rows > 1024:
+                self.sent.append(0)
+            self.sent[-1] += rows
+            send = self.send.at[len(self.sent) - 1]
         copy = pltpu.make_async_remote_copy(
             src_ref=src,
             dst_ref=dst,
-            send_sem=self.send.at[k],
-            recv_sem=self.recv.at[k],
+            send_sem=send,
+            recv_sem=self.recv.at[self.used],
             device_id=where,
             device_id_type=MESH,
         )
+        self.used += 1
         copy.start()
-        self.open.append(copy)
         return copy
 
-    def drain(self):
-        for copy in self.open:
-            copy.wait_send()
+    def drain(self, rows_of_4k):
+        for k, count in enumerate(self.sent):
+            some = rows_of_4k.at[pl.ds(0, count)]
+            pltpu.make_async_copy(some, some, self.send.at[k]).wait()
 
 
 def owner_bounds(counts_ref):
@@ -130,7 +134,7 @@
     T, B = slice(0, 16), slice(16, 32)
 
     def __init__(self, ref, go, where, out, sem):
-        self.ref, self.go, self.out, self.sem, self.written = ref, go, out, sem, []
+        self.ref, self.go, self.out, self.sem = ref, go, out, sem
         self.x, self.y, self.c, _ = where
         self.xr, self.xl, self.xo = ((self.x + d) % 4 for d in (1, 3, 2))
         self.yr, self.yl, self.yo = ((self.y + d) % 4 for d in (1, 3, 2))
@@ -150,10 +154,7 @@
             self.write((a, b, 1 - self.c, rows, cols))
 
     def write(self, piece):
-        k = len(self.written)
-        copy = pltpu.make_async_copy(self.ref.at[piece], self.out.at[piece], self.sem.at[k])
-        copy.start()
-        self.written.append(copy)
+        pltpu.make_async_copy(self.ref.at[piece], self.out.at[piece], self.sem).start()
 
     def same(self, piece, where):
         ref = self.ref.at[piece]
@@ -222,11 +223,119 @@
         self.from_partner(6, 8)
 
     def close(self):
-        for copy in self.written:
-            copy.wait()
-
-
-N_COPIES = 140
+        pltpu.make_async_copy(self.ref, self.out, self.sem).wait()
+
+
+class Flow(Spread):
+    def part(self, h, i, j, rows):
+        if h == 0:
+            return (i, j, self.c, rows, self.LO)
+        return (j, i, self.c, rows, self.HI)
+
+    def send(self, h, axis, step, i, j, rows):
+        along_x = (h == 0) == (axis == 0)
+        n = self.x if along_x else self.y
+        return self.same(
+            self.part(h, i, j, rows), {"dp_0" if along_x else "dp_1": (n + step) % 4}
+        )
+
+    def start(self):
+        every = slice(None)
+        self.n = ((self.x, self.y), (self.y, self.x))
+        self.hop1, self.own, self.side, self.opp = {}, {}, {}, {}
+        for h in range(2):
+            i, j = self.n[h]
+            for step in (1, 3):
+                self.hop1[h, step] = self.send(h, 0, step, i, j, every)
+        for h in range(2):
+            i, j = self.n[h]
+            for step in (1, 3):
+                self.own[h, step] = self.send(h, 1, step, i, j, every)
+
+    def sides(self):
+        every = slice(None)
+        self.hop2 = {}
+        for h in range(2):
+            i, j = self.n[h]
+            for step, rows in ((1, self.T), (3, self.B)):
+                self.hop1[h, step].wait_recv()
+                k = (i - step) % 4
+                self.hop2[h, step] = self.send(h, 0, step, k, j, rows)
+                for way in (1, 3):
+                    self.side[h, step, way] = self.send(h, 1, way, k, j, every)
+
+    def owns_on(self):
+        self.own_on = {}
+        for h in range(2):
+            i, j = self.n[h]
+            for step, rows in ((1, self.T), (3, self.B)):
+                self.own[h, step].wait_recv()
+                self.own_on[h, step] = self.send(h, 1, step, i, (j - step) % 4, rows)
+
+    def opposites(self):
+        every = slice(None)
+        for h in range(2):
+            i, j = self.n[h]
+            for step, rows in ((1, self.T), (3, self.B)):
+                self.hop2[h, step].wait_recv()
+                for way in (1, 3):
+                    self.opp[h, step, way] = self.send(h, 1, way, (i + 2) % 4, j, rows)
+            self.across(self.part(h, every, j, every))
+
+    def sides_on(self):
+        self.side_on = {}
+        for h in range(2):
+            i, j = self.n[h]
+            for step in (1, 3):
+                for way, rows in ((1, self.T), (3, self.B)):
+                    self.side[h, step, way].wait_recv()
+                    self.side_on[h, step, way] = self.send(
+                        h, 1, way, (i - step) % 4, (j - way) % 4, rows
+                    )
+
+    def opposites_on(self):
+        every = slice(None)
+        self.opp_on = {}
+        for h in range(2):
+            i, j = self.n[h]
+            for step, rows in ((1, self.T), (3, self.B)):
+                self.opp[h, step, step].wait_recv()
+                self.opp_on[h, step] = self.send(
+                    h, 1, step, (i + 2) % 4, (j - step) % 4, rows
+                )
+        for h in range(2):
+            i, j = self.n[h]
+            for step in (1, 3):
+                self.opp[h, step, 4 - step].wait_recv()
+            for way in (1, 3):
+                self.across(self.part(h, every, (j - way) % 4, every))
+
+    def finals(self):
+        every = slice(None)
+        self.from_partner(0, 2)
+        for h in range(2):
+            i, j = self.n[h]
+            far = (j + 2) % 4
+            for step in (1, 3):
+                self.own_on[h, step].wait_recv()
+            self.across(self.part(h, i, far, every))
+        for h in range(2):
+            i, j = self.n[h]
+            far = (j + 2) % 4
+            for step in (1, 3):
+                for way in (1, 3):
+                    self.side_on[h, step, way].wait_recv()
+                self.across(self.part(h, (i - step) % 4, far, every))
+        self.from_partner(2, 6)
+        for h in range(2):
+            i, j = self.n[h]
+            for step in (1, 3):
+                self.opp_on[h, step].wait_recv()
+            self.across(self.part(h, (i + 2) % 4, (j + 2) % 4, every))
+        self.from_partner(6, 14)
+
+
+N_COPIES = 131
 
 
 def step_kernel(
@@ -369,7 +478,7 @@
         copy.wait_recv()
     forward(zo)
 
-    sent = [go_to(lg, LR.at[z], {"mp": (z + d) % 4}) for d in (1, 2, 3)]
+    sent = [go_to(lg, LR.at[z], {"mp": (z + d) % 4}, bulk.at[8]) for d in (1, 2, 3)]
     LR[z] = lg[...]
     for copy in sent:
         copy.wait_recv()
@@ -625,8 +734,8 @@
     grad_ref[:, HI] = upper
     GA[x, y, c, :, LO] = lower.astype(BF16)
     GA[x, y, c, :, HI] = upper.astype(BF16)
-    ga = Spread(GA, go_to, (x, y, c, z), ga_out, wsem.at[1])
-    ga.first()
+    ga = Flow(GA, go_to, (x, y, c, z), ga_out, wsem.at[1])
+    ga.start()
     both = lower * lower + upper * upper
     both = jnp.sum(both.reshape(4, 8, 1024), axis=0)
     for t in range(8):
@@ -647,7 +756,7 @@
     put_grad = pltpu.make_async_copy(grad_ref, grad_out, local.at[10])
     put_grad.start()
     NR[me] = ns[...]
-    ga.second()
+    ga.sides()
 
     heard = idsend.at[pl.ds(0, 127)]
     pltpu.make_async_copy(heard, heard, bulk.at[1]).wait()
@@ -661,12 +770,14 @@
         lined[side] = line
     acc[...] = jnp.zeros_like(acc)
     aa.last()
-    ga.third()
+    ga.owns_on()
+    ga.opposites()
+    ga.sides_on()
     many = arrived_ref.at[pl.ds(0, 127)]
     pltpu.make_async_copy(many, many, bulk.at[5]).wait()
-    rows_of_table(0, 5)
-    ga.fourth()
-    rows_of_table(5, 8)
+    rows_of_table(0, 4)
+    ga.opposites_on()
+    rows_of_table(4, 8)
     put_sums = pltpu.make_async_copy(acc, sums_out, local.at[11])
     put_sums.start()
     lot = NR.at[pl.ds(0, 127)]
@@ -677,15 +788,15 @@
     scale_ref[...] = jnp.broadcast_to(scale, (8, 128))
     put_scale = pltpu.make_async_copy(scale_ref, scale_out, local.at[12])
     put_scale.start()
-    ga.fifth()
-    ga.last()
+    ga.finals()
     pltpu.make_async_copy(lot, lot, bulk.at[6]).wait()
     pltpu.make_async_copy(many, many, bulk.at[4]).wait()
     pltpu.make_async_copy(heard, heard, bulk.at[0]).wait()
     put_grad.wait()
     put_sums.wait()
     put_scale.wait()
-    cp.drain()
+    pltpu.make_async_copy(LR.at[0:3], LR.at[0:3], bulk.at[8]).wait()
+    cp.drain(W)
     aa.close()
     ga.close()
 
@@ -810,7 +921,7 @@
             V(whole, BF16), V(whole, BF16), V((128, 2048), F32), V((128, 16, 128), BF16),
             V((1, 128), F32), V((128, 1, 128), F32), V((4, 4, 32, 2048), BF16),
             V((2048, 128), BF16), V((1, 2048), F32), V((2048, 128), F32),
-            DMA((N_COPIES,)), DMA((N_COPIES,)), DMA((8,)), DMA((13,)), DMA((2, 16)),
+            DMA((4,)), DMA((N_COPIES,)), DMA((9,)), DMA((13,)), DMA((2,)),
         ],
         compiler_params=pltpu.CompilerParams(
             has_side_effects=True, vmem_limit_bytes=63 * 1024 * 1024, collective_id=0

time: 109 us -> 105 us (0.963)
  Pallas kernels: 108 us -> 104 us
    pallas_call x1, Pallas kernels: 98.5 us -> 95 us  [body(): pl.pallas_call(step_kernel, out_shape=(shape(whole, BF16), shape(whole, B...]
where the time goes in v5:
time: 105 us
  Pallas kernels  104 us (99%)
    pallas_call x1, Pallas kernels, body(): pl.pallas_call(step_kernel, out_shape=(shape(whole, BF16), shape(whole, B...  95 us
    pallas_call x1, Pallas kernels, body(): pl.pallas_call(finish_kernel, out_shape=(shape((64, 4096), F32), shape((3...  9.22 us

profile of v5, /device:TPU:1, one launch (start us, length us, event | category | flops | bytes accessed | tf_op | source)
XLA Modules:
  0.0 105.0 jit_solution(9775889785027257787)
XLA Ops:
  0.6 95.0 %step.1 = (bf16[4,4,2,32,2048]{4,3,2,1,0:T(8,128)(2,1)}, bf16[4,4,2,32,2048]{4,3,2,1,0:T(8,128)(2,1)}, f32[128,2048]{1,0:T(8,128)}, f32[8,128]{1,0:T(8,128)}, f32[32,2048]{1,0:T(8,128)}) custom-call(s32[16,256]{1,0:T(8,128)} %bitcast.19, s32[1,128]{1,0:T(1,128)} %counts_any.1, bf16[128,2048]{1,0:T(8,128)(2,1)} %bitcast.18, s32[32,128]{1,0:T(8,128)} %bitcast.20, ...), custom_call_target="tpu_custom_call" | custom-call | tf_op jit(solution)/shard_map/step/pallas_call | solution.py:897
  95.7 9.2 %finish.1 = (f32[64,4096]{1,0:T(8,128)}, f32[32,128]{1,0:T(8,128)}, f32[32,2048]{1,0:T(8,128)}, bf16[1024,2048]{1,0:T(8,128)(2,1)}) custom-call(f32[128,2048]{1,0:T(8,128)} %get-tuple-element.13.sums_any, f32[8,128]{1,0:T(8,128)} %get-tuple-element.14.scale_ref, f32[64,4096]{1,0:T(8,128)} %bitcast.17, f32[32,128]{1,0:T(8,128)} %bitcast.21, ...), custom_call_target="tpu_custom_call" | custom-call | tf_op jit(solution)/shard_map/finish/pallas_call | solution.py:942

commit v6 on v5

--- a/solution.py
+++ b/solution.py
@@ -347,7 +347,7 @@
     W, A, idsend, G, fac, hidden, dact, pacc, lg, LR, DL, gb, go, sv, rv,
     ZS, Df, ZRL, ZRR, ZL, ZR, DPL,
     R0, SB, RL, RV, Q, RL2, RV2,
-    GA, AA, acc, slots, ns, NR, SC, slab, wout, strided,
+    GA, AA, acc, slots, ns, NR, GT, slab, wout, strided,
     ssem, rsem, bulk, local, wsem,
 ):
     x, y, c, z = position()
@@ -457,11 +457,17 @@
             line = jnp.sum(pacc[128 * s : 128 * s + 128, :].T, axis=0, keepdims=True)
             lg[pl.ds(src * 2 + s, 1), :] = line
 
+    def turn(src):
+        rows = pl.ds(pl.multiple_of(src * 256, 256), 256)
+        for t in range(4):
+            GT[256 * t : 256 * t + 256, rows] = G[rows, 256 * t : 256 * t + 256].T
+
     right[0].wait_recv()
     f0 = go_to(block(zl, 0), block(zl, 0), {"mp": zr})
     left[2].wait_recv()
     f2 = go_to(block(zr, 2), block(zr, 2), {"mp": zl})
     forward(z)
+    turn(z)
     right[1].wait_recv()
     f1 = go_to(block(zl, 1), block(zl, 1), {"mp": zr})
     left[3].wait_recv()
@@ -473,6 +479,7 @@
     left[0].wait_recv()
     left[1].wait_recv()
     forward(zr)
+    turn(zl)
     aa.third()
     for copy in (f0, f1, f2, f3):
         copy.wait_recv()
@@ -480,6 +487,8 @@
 
     sent = [go_to(lg, LR.at[z], {"mp": (z + d) % 4}, bulk.at[8]) for d in (1, 2, 3)]
     LR[z] = lg[...]
+    turn(zr)
+    turn(zo)
     for copy in sent:
         copy.wait_recv()
     logit = (LR[0] + LR[1]) + (LR[2] + LR[3])
@@ -535,18 +544,17 @@
 
         def tile(t, carry):
             cols = pl.ds(pl.multiple_of(t * 1024, 1024), 1024)
-            g = mm(G[:, pl.ds(at, 256)], dact[:, cols], 0, 0)
+            g = mm(GT[pl.ds(at, 256), :], dact[:, cols], 1, 0)
             fac[xi, :, :, :, cols] = g.reshape(4, 2, 32, 1024)
-            SC[xi, :, :, cols] = fac[xi, :, 1 - c, :, cols].astype(BF16)
             return carry
 
         lax.fori_loop(0, 2, tile, 0)
-        to_core[tag] = go_to(SC.at[xi], R0.at[xi], partner)
+        to_core[tag] = go_to(fac.at[xi, :, 1 - c], R0.at[xi], partner)
 
     def chip_sum(xi, tag):
         to_core[tag].wait_recv()
         for yi in range(4):
-            s = R0[xi, yi].astype(F32) + fac[xi, yi, c]
+            s = R0[xi, yi] + fac[xi, yi, c]
             fac[xi, yi, c] = s
             SB[xi, yi] = s.astype(BF16)
 
@@ -771,13 +779,14 @@
     acc[...] = jnp.zeros_like(acc)
     aa.last()
     ga.owns_on()
+    many = arrived_ref.at[pl.ds(0, 127)]
+    pltpu.make_async_copy(many, many, bulk.at[5]).wait()
+    rows_of_table(0, 2)
     ga.opposites()
     ga.sides_on()
-    many = arrived_ref.at[pl.ds(0, 127)]
-    pltpu.make_async_copy(many, many, bulk.at[5]).wait()
-    rows_of_table(0, 4)
+    rows_of_table(2, 5)
     ga.opposites_on()
-    rows_of_table(4, 8)
+    rows_of_table(5, 8)
     put_sums = pltpu.make_async_copy(acc, sums_out, local.at[11])
     put_sums.start()
     lot = NR.at[pl.ds(0, 127)]
@@ -915,13 +924,13 @@
             V((3, 256, 1024), BF16), V((2, 128, 1024), F32),
             V((128, 1024), BF16), V((128, 1024), BF16),
             V((256, 1024), BF16), V((256, 1024), BF16), V((256, 1024), F32),
-            V((4, 4, 32, 2048), BF16), V((4, 4, 32, 2048), BF16),
+            V((4, 4, 32, 2048), F32), V((4, 4, 32, 2048), BF16),
             V((2, 2, 2, 32, 1024), BF16), V((2, 2, 4, 32, 1024), BF16),
             V((2, 4, 32, 1024), F32), V((2, 2, 16, 1024), F32), V((2, 2, 32, 1024), F32),
             V(whole, BF16), V(whole, BF16), V((128, 2048), F32), V((128, 16, 128), BF16),
-            V((1, 128), F32), V((128, 1, 128), F32), V((4, 4, 32, 2048), BF16),
+            V((1, 128), F32), V((128, 1, 128), F32), V((1024, 1024), BF16),
             V((2048, 128), BF16), V((1, 2048), F32), V((2048, 128), F32),
-            DMA((4,)), DMA((N_COPIES,)), DMA((9,)), DMA((13,)), DMA((2,)),
+            DMA((5,)), DMA((N_COPIES,)), DMA((9,)), DMA((13,)), DMA((2,)),
         ],
         compiler_params=pltpu.CompilerParams(
             has_side_effects=True, vmem_limit_bytes=63 * 1024 * 1024, collective_id=0

time: 105 us -> 105 us (level)
  no operation moved by 1% of the time
where the time goes in v6:
time: 105 us
  Pallas kernels  104 us (99%)
    pallas_call x1, Pallas kernels, body(): pl.pallas_call(step_kernel, out_shape=(shape(whole, BF16), shape(whole, B...  94.5 us
    pallas_call x1, Pallas kernels, body(): pl.pallas_call(finish_kernel, out_shape=(shape((64, 4096), F32), shape((3...  9.22 us

profile of v6, /device:TPU:1, one launch (start us, length us, event | category | flops | bytes accessed | tf_op | source)
XLA Modules:
  0.0 104.6 jit_solution(16588136710521204510)
XLA Ops:
  0.6 94.5 %step.1 = (bf16[4,4,2,32,2048]{4,3,2,1,0:T(8,128)(2,1)}, bf16[4,4,2,32,2048]{4,3,2,1,0:T(8,128)(2,1)}, f32[128,2048]{1,0:T(8,128)}, f32[8,128]{1,0:T(8,128)}, f32[32,2048]{1,0:T(8,128)}) custom-call(s32[16,256]{1,0:T(8,128)} %bitcast.19, s32[1,128]{1,0:T(1,128)} %counts_any.1, bf16[128,2048]{1,0:T(8,128)(2,1)} %bitcast.18, s32[32,128]{1,0:T(8,128)} %bitcast.20, ...), custom_call_target="tpu_custom_call" | custom-call | tf_op jit(solution)/shard_map/step/pallas_call | solution.py:906
  95.2 9.2 %finish.1 = (f32[64,4096]{1,0:T(8,128)}, f32[32,128]{1,0:T(8,128)}, f32[32,2048]{1,0:T(8,128)}, bf16[1024,2048]{1,0:T(8,128)(2,1)}) custom-call(f32[128,2048]{1,0:T(8,128)} %get-tuple-element.13.sums_any, f32[8,128]{1,0:T(8,128)} %get-tuple-element.14.scale_ref, f32[64,4096]{1,0:T(8,128)} %bitcast.17, f32[32,128]{1,0:T(8,128)} %bitcast.21, ...), custom_call_target="tpu_custom_call" | custom-call | tf_op jit(solution)/shard_map/finish/pallas_call | solution.py:951
